TPU v7x, 16 devices: a whole 2x2x2 slice. The times are simulated.
16 devices in a mesh: model: 2 (over z), sub: 2 (over y), data: 4 (over x, core).
Axes of the slice: x: 2, y: 2, z: 2, core: 2. Of those that a mesh axis runs over, the one named last changes fastest.
Arguments:
- images: bfloat16 [16, 576, 384], P(('model', 'sub', 'data'))
- targets: bfloat16 [16, 576, 384], P(('model', 'sub', 'data'))
- w_in: float32 [16, 384, 1536], replicated
- w_out: float32 [16, 1536, 384], replicated
Outputs:
- output 1: float32 [16, 384, 1536], replicated
- output 2: float32 [16, 1536, 384], replicated
- output 3: float32 [], replicated
All inputs are finite; a program needn't handle non-finite values.
Results may differ from a plain program's by a relative error of at most 0.00699408.
Values are sent between devices in bfloat16 or wider.
A program may use at most 1 GiB of HBM per device.

v0:
```python
import jax
import jax.numpy as jnp
import math
from jax import lax
from jax.sharding import PartitionSpec as P

RHO_REL = 0.1
LEARN_RATE = 8.0
SQRT_HALF = 0.7071067811865476
INV_SQRT_2PI = 0.3989422804014327


def gelu_fn(pre_act):
    return 0.5 * pre_act * (1.0 + lax.erf(pre_act * SQRT_HALF))


def gelu_slope(pre_act):
    cdf_part = 0.5 * (1.0 + lax.erf(pre_act * SQRT_HALF))
    return cdf_part + pre_act * INV_SQRT_2PI * jnp.exp(-0.5 * pre_act * pre_act)


def forward(x_rows, in_list, out_list):
    hidden = x_rows
    saved_acts = []
    for layer_idx in range(len(in_list)):
        pre_act = jnp.dot(hidden, in_list[layer_idx], preferred_element_type=jnp.float32).astype(jnp.bfloat16)
        post_act = gelu_fn(pre_act.astype(jnp.float32)).astype(jnp.bfloat16)
        mlp_out = jnp.dot(post_act, out_list[layer_idx], preferred_element_type=jnp.float32)
        saved_acts.append((hidden, pre_act, post_act))
        hidden = (hidden.astype(jnp.float32) + mlp_out).astype(jnp.bfloat16)
    return hidden, saved_acts


def backward(d_top, saved_acts, in_list, out_list):
    d_hidden = d_top
    grads_in = []
    grads_out = []
    for layer_idx in reversed(range(len(saved_acts))):
        hidden, pre_act, post_act = saved_acts[layer_idx]
        grads_out.append(jnp.einsum('tf,td->fd', post_act, d_hidden, preferred_element_type=jnp.float32))
        d_act = jnp.einsum('td,fd->tf', d_hidden, out_list[layer_idx], preferred_element_type=jnp.float32)
        d_pre = (d_act * gelu_slope(pre_act.astype(jnp.float32))).astype(jnp.bfloat16)
        grads_in.append(jnp.einsum('td,tf->df', hidden, d_pre, preferred_element_type=jnp.float32))
        if layer_idx > 0:
            back_part = jnp.einsum('tf,df->td', d_pre, in_list[layer_idx], preferred_element_type=jnp.float32)
            d_hidden = (d_hidden.astype(jnp.float32) + back_part).astype(jnp.bfloat16)
    return grads_in[::-1], grads_out[::-1]


def top_grad(top_hidden, y_rows, inv_count):
    resid_err = top_hidden.astype(jnp.float32) - y_rows.astype(jnp.float32)
    return 0.5 * jnp.sum(resid_err * resid_err), (resid_err * inv_count).astype(jnp.bfloat16)


def solution(mesh):
    mesh_axes = tuple(mesh.axis_names)
    dev_count = math.prod([mesh.shape[axis_name] for axis_name in mesh_axes])
    batch_spec = P(mesh_axes, None, None)

    def local_step(images, targets, w_in, w_out):
        layers, model_dim, hidden_dim = w_in.shape
        tok_local = images.shape[0] * images.shape[1]
        inv_count = 1.0 / (tok_local * dev_count * model_dim)
        radius = RHO_REL * math.sqrt(layers * hidden_dim + model_dim)
        x_rows = images.reshape(tok_local, model_dim)
        y_rows = targets.reshape(tok_local, model_dim)
        w_in_bf = w_in.astype(jnp.bfloat16)
        w_out_bf = w_out.astype(jnp.bfloat16)
        in_list = [w_in_bf[layer_idx] for layer_idx in range(layers)]
        out_list = [w_out_bf[layer_idx] for layer_idx in range(layers)]
        top_hidden, saved_acts = forward(x_rows, in_list, out_list)
        _, d_top = top_grad(top_hidden, y_rows, inv_count)
        grads_in, grads_out = backward(d_top, saved_acts, in_list, out_list)
        grads_in, grads_out = lax.psum((grads_in, grads_out), mesh_axes)
        norm_sq = sum(jnp.sum(grad_part * grad_part) for grad_part in grads_in + grads_out)
        step_scale = radius / jnp.sqrt(norm_sq)
        pert_in = [(w_in[layer_idx] + step_scale * grads_in[layer_idx]).astype(jnp.bfloat16) for layer_idx in range(layers)]
        pert_out = [(w_out[layer_idx] + step_scale * grads_out[layer_idx]).astype(jnp.bfloat16) for layer_idx in range(layers)]
        top_pert, saved_pert = forward(x_rows, pert_in, pert_out)
        loss_local, d_pert = top_grad(top_pert, y_rows, inv_count)
        grads2_in, grads2_out = backward(d_pert, saved_pert, pert_in, pert_out)
        grads2_in, grads2_out, loss_total = lax.psum((grads2_in, grads2_out, loss_local), mesh_axes)
        new_in = w_in - LEARN_RATE * jnp.stack(grads2_in)
        new_out = w_out - LEARN_RATE * jnp.stack(grads2_out)
        return new_in, new_out, loss_total * inv_count

    return jax.shard_map(local_step, mesh=mesh, in_specs=(batch_spec, batch_spec, P(), P()), out_specs=(P(), P(), P()), check_vma=False)
```

profile of v0, /device:TPU:1, one launch (start us, length us, event | category | flops | bytes accessed | tf_op | source)
XLA Modules:
  0.0 2946.8 jit_solution(1228890018230653134)
XLA Ops:
  7.2 21.6 convert_element_type.916
  28.8 7.9 copy-done
  36.7 8.1 convert_element_type.912
  147.8 5.6 fusion.147
  179.2 5.6 fusion.129
  216.1 6.0 fusion.460
  289.3 5.7 fusion.66
  295.0 5.6 fusion.475
  370.5 6.0 convolution_bitcast_fusion.32
  386.6 37.0 %copy.53 = f32[16,384,1536]{1,2,0:T(8,128)} copy(f32[16,384,1536]{2,1,0:T(8,128)} %param.6) | data formatting | bytes 75497472 | tf_op args[2]
  423.6 963.4 %all-reduce.7.cloned.1.call-done = (f32[384,1536]{0,1:T(8,128)}, f32[384,1536]{0,1:T(8,128)}, f32[384,1536]{0,1:T(8,128)}, f32[384,1536]{0,1:T(8,128)}, f32[384,...) async-done(((f32[384,1536]{0,1:T(8,128)}, ...) | async-done | bytes 75497488 | tf_op jit(solution)/shard_map/psum | solution.py:74
  1465.3 18.4 fusion.320
  1483.8 13.3 fusion.329
  1497.1 18.3 fusion.289
  1515.4 9.4 fusion.307
  1584.9 5.6 multiply_reduce_fusion.32
  1590.5 5.9 fusion.282
  1596.5 5.7 convolution_bitcast_fusion
  1734.5 5.9 convolution_bitcast_fusion.31
  1745.7 34.6 %psum.519 = f32[]{:T(128)} all-reduce(f32[]{:T(128)S(6)} %mul.1512), channel_id=1, replica_groups=mesh['model'=2,'sub'=2,'data'=4] {'model','sub','data'}, use_global_device_ids=true, to_apply=%region_97.0 | all-reduce | flops 1 | bytes 8 | tf_op jit(solution)/shard_map/psum | solution.py:82
  1781.0 965.9 %all-reduce.5.cloned.1.call-done = (f32[1,384,1536]{1,2,0:T(8,128)}, f32[1,384,1536]{1,2,0:T(8,128)}, f32[1,384,1536]{1,2,0:T(8,128)}, f32[1,384,1536]{1,2,0:T(8...) async-done(((f32[1,384,1536]{1,2,0:T(8,128)}, ...) | async-done | bytes 75497488 | tf_op jit(solution)/shard_map/psum | solution.py:82
  2787.0 37.7 %multiply_subtract_fusion.1 = f32[16,384,1536]{1,2,0:T(8,128)} fusion(f32[16,384,1536]{1,2,0:T(8,128)} %copy.53, f32[16,384,1536]{1,2,0:T(8,128)} %constant_dynamic-update-slice_fusion), kind=kLoop, calls=%fused_computation.1 | loop fusion | flops 18874368 | bytes 113246208 | tf_op jit(solution)/shard_map/sub | solution.py:83
  2824.7 36.9 %copy.54 = f32[16,384,1536]{2,1,0:T(8,128)} copy(f32[16,384,1536]{1,2,0:T(8,128)} %multiply_subtract_fusion.1) | data formatting | bytes 75497472
  2900.9 37.7 %multiply_subtract_fusion = f32[16,1536,384]{2,1,0:T(8,128)} fusion(f32[16,1536,384]{2,1,0:T(8,128)} %param.7, f32[16,1536,384]{2,1,0:T(8,128)} %constant_dynamic-update-slice_fusion.16), kind=kLoop, calls=%fused_computation | loop fusion | flops 18874368 | bytes 113246208 | tf_op jit(solution)/shard_map/sub | solution.py:84
  (771 shorter events, 638.8 us)
Async XLA Ops:
  7.2 1379.9 %all-reduce.7.cloned.1.call-start = ((), (), s32[]{:S(2)}) async-start(), calls=%async_computation.1 | async-start | bytes 150994944 | tf_op jit(solution)/shard_map/psum | solution.py:74
  7.2 29.5 %copy-start = (f32[16,384,1536]{2,1,0:T(8,128)S(1)}, f32[16,384,1536]{2,1,0:T(8,128)}, u32[]{:S(2)}) copy-start(f32[16,384,1536]{2,1,0:T(8,128)} %param.6) | copy-start | bytes 113246208
  36.7 8.1 copy-start.76
  123.6 22.3 slice-start
  126.1 19.7 slice-start.1
  130.4 15.4 slice-start.2
  133.0 12.8 slice-start.3
  138.0 20.9 slice-start.5
  140.6 18.3 slice-start.6
  145.9 13.1 slice-start.7
  147.8 11.2 slice-start.8
  147.8 11.2 slice-start.9
  386.6 2360.3 %all-reduce.5.cloned.1.call-start = ((), (), s32[]{:S(2)}) async-start(), calls=%async_computation | async-start | bytes 150994944 | tf_op jit(solution)/shard_map/psum | solution.py:82
  1465.3 18.5 copy-start.75
  1497.1 32.0 %copy-start.78 = (bf16[1536,384]{1,0:T(8,128)(2,1)}, bf16[1536,384]{1,0:T(8,128)(2,1)S(1)}, u32[]{:S(2)}) copy-start(bf16[1536,384]{1,0:T(8,128)(2,1)S(1)} %get-tuple-element.94) | copy-start | bytes 3538948
  1497.1 18.3 copy-start.73
  1515.4 9.4 copy-start.74
  1515.4 9.4 copy-start.77
  1524.9 10.4 copy-start.108
  1524.9 14.3 copy-start.110
  1524.9 18.3 copy-start.112
  1524.9 21.2 copy-start.114
  1524.9 24.1 copy-start.118
  2824.7 36.9 %copy-start.207 = (f32[1,1536,384]{2,1,0:T(8,128)S(1)}, f32[1,1536,384]{2,1,0:T(8,128)}, u32[]{:S(2)}) copy-start(f32[1,1536,384]{2,1,0:T(8,128)} %get-tuple-element.22) | copy-start | bytes 7077892
  (248 other events, 715.5 us)
Sparse Core Ops, SparseCore 0:
  386.7 1000.2 all-reduce.6
  1745.2 1001.5 all-reduce.4
where the time goes:
time: 2960 us; the launch traced here: 2950 us
  waiting for transfers between devices  1930 us (65%)
  matrix products  533 us (18%)
  other arithmetic  222 us (8%)
  local copies, waits for them, and re-layouts  187 us (6%)
  between operations  40.1 us (1%)
  blocking collectives  34.6 us (1%)
    psum x1, waiting for transfers between devices, local_step(): lax.psum((grads2_in, grads2_out, loss_local), mesh_axes)  966 us
    psum x1, waiting for transfers between devices, local_step(): grads_in, grads_out = lax.psum((grads_in, grads_out), mesh_axes)  963 us
    unnamed x572, local copies, waits for them, and re-layouts  184 us
    dot_general x32, matrix products, backward(): jnp.einsum('tf,td->fd', post_act, d_hidden, preferred_element_type=jnp.fl...  135 us
    dot_general x30, matrix products, backward(): jnp.einsum('td,fd->tf', d_hidden, out_list[layer_idx], preferred_element_...  112 us
    dot_general x32, matrix products, backward(): jnp.einsum('td,tf->df', hidden, d_pre, preferred_element_type=jnp.float32)  95.2 us
    dot_general x32, matrix products, forward(): jnp.dot(hidden, in_list[layer_idx], preferred_element_type=jnp.float32)  71.5 us
    dot_general x32, matrix products, forward(): jnp.dot(post_act, out_list[layer_idx], preferred_element_type=jnp.float32)  70.6 us
  transfers between devices with their start and end apart: 2, of which 2 were waited for; matrix products, arithmetic and copies ran while one was open for 1% of the time, Pallas kernels for 0%

commit v1 on v0

v1 whole, which is shorter than its diff:
```python
import functools
import math

import jax
import jax.numpy as jnp
from jax import lax
from jax.experimental import pallas as pl
from jax.experimental.pallas import tpu as pltpu
from jax.sharding import PartitionSpec as P

MESH = pl.DeviceIdType.MESH
RHO_REL = 0.1
LEARN_RATE = 8.0
SQRT_HALF = 0.7071067811865476
INV_SQRT_2PI = 0.3989422804014327

CHIPS = 8
LAYERS = 16
D = 384
F = 1536
T = 576
ROWS = CHIPS * T
FT = 768
KB_ROWS = 512
KB_FT = 512

f32, bf16 = jnp.float32, jnp.bfloat16
NN = (((1,), (0,)), ((), ()))
NT = (((1,), (1,)), ((), ()))
V = pl.BlockSpec(memory_space=pltpu.VMEM)
ANY = pl.BlockSpec(memory_space=pl.ANY)
DMA = pltpu.SemaphoreType.DMA


def dot(a, b, dims=NN):
    return lax.dot_general(a, b, dims, preferred_element_type=f32)


def cdf(x):
    return 0.5 * (1.0 + lax.erf(x * SQRT_HALF))


def slope_tail(x):
    return x * INV_SQRT_2PI * jnp.exp(-0.5 * x * x)


class Place:
    def __init__(self):
        self.z, self.y, data = lax.axis_index("model"), lax.axis_index("sub"), lax.axis_index("data")
        self.x, self.core = data // 2, data % 2
        self.chip = self.z * 4 + self.y * 2 + self.x
        self.coords = (self.x, self.y, self.z)

    def device(self, chip, core):
        return (chip // 4, (chip // 2) % 2, (chip % 2) * 2 + core)

    def partner(self):
        return self.device(self.chip, 1 - self.core)

    def flipped(self, dims):
        x, y, z = ((1 - v) if d in dims else v for d, v in enumerate(self.coords))
        return z * 4 + y * 2 + x

    def neighbour(self, dim):
        return self.device(self.flipped((dim,)), self.core)

    def same_core_peers(self):
        return [self.device(self.flipped(s), self.core) for s in SUBSETS[1:]]

    def all_peers(self):
        return self.same_core_peers() + [self.device(self.flipped(s), 1 - self.core) for s in SUBSETS]


SUBSETS = ((), (0,), (1,), (0, 1), (2,), (0, 2), (1, 2), (0, 1, 2))


def meet(peers):
    barrier = pltpu.get_barrier_semaphore()
    for peer in peers:
        pl.semaphore_signal(barrier, inc=1, device_id=peer, device_id_type=MESH)
    pl.semaphore_wait(barrier, len(peers))


def remote(src, dst, send_sem, recv_sem, device):
    return pltpu.make_async_remote_copy(
        src_ref=src, dst_ref=dst, send_sem=send_sem, recv_sem=recv_sem, device_id=device, device_id_type=MESH
    )


class Gather:
    def __init__(self, at, tensors, send, recv, pair_send, pair_recv):
        self.at, self.tensors = at, tensors
        self.send, self.recv, self.pair_send, self.pair_recv = send, recv, pair_send, pair_recv
        self.pairs, self.copies = [], {}

    def messages(self, dim):
        a, b = (dim - 1) % 3, (dim - 2) % 3
        return [(dim, ()), (a, ()), (b, ()), (a, (a,)), (b, (b,)), (b, (a,)), (b, (a, b))]

    def make(self, part, flips, send, recv, device):
        layer = self.at.flipped(flips) * 2 + self.at.core
        out = []
        for i, (own, slots) in enumerate(self.tensors):
            n = slots.shape[1] // 3
            rows = pl.ds(part * n, n)
            dst = slots.at[layer, rows, :]
            src = own.at[rows, :] if not flips else dst
            out.append(remote(src, dst, send.at[i], recv.at[i], device))
        return out

    def link(self, dim, slot):
        if (dim, slot) not in self.copies:
            part, flips = self.messages(dim)[slot]
            self.copies[dim, slot] = self.make(
                part, flips, self.send.at[dim, slot], self.recv.at[dim, slot], self.at.neighbour(dim)
            )
        return self.copies[dim, slot]

    def hand_over(self, part, flips):
        i = len(self.pairs)
        copies = self.make(part, flips, self.pair_send.at[i], self.pair_recv.at[i], self.at.partner())
        for c in copies:
            c.start()
        self.pairs.append(copies)

    def start(self):
        for slot in range(3):
            for dim in range(3):
                for c in self.link(dim, slot):
                    c.start()
        for part in range(3):
            self.hand_over(part, ())

    def run(self):
        relay = {0: (3, 4), 1: (5,), 3: (6,)}
        for slot in range(7):
            for dim in range(3):
                for c in self.link(dim, slot):
                    c.wait_recv()
            for later in relay.get(slot, ()):
                for dim in range(3):
                    for c in self.link(dim, later):
                        c.start()
            for dim in range(3):
                part, flips = self.messages(dim)[slot]
                self.hand_over(part, tuple(sorted(set(flips) ^ {dim})))
        for copies in self.pairs:
            for c in copies:
                c.wait_recv()

    def finish(self):
        for copies in [*self.pairs, *self.copies.values()]:
            for c in copies:
                c.wait_send()


GATHER_SEMS = [DMA((3, 7, 2)), DMA((3, 7, 2)), DMA((24, 2)), DMA((24, 2))]


def local_kernel(perturbed, inv_count, *refs):
    if perturbed:
        (x_ref, y_ref, wi_own, wo_own, h_out, d_out, pi_out, po_out, u_hbm, loss_out,
         wi, wo, hs, ds, mid, acc, us, hsend, hrecv, dsend, drecv, usem, wsem,
         gs, gr, ps, pr, lbuf, lsend, lrecv) = refs
    else:
        (x_ref, y_ref, wi_hbm, wo_hbm, h_out, d_out, pi_out, po_out, u_hbm,
         wi, wo, hs, ds, mid, acc, us, hsend, hrecv, dsend, drecv, usem, wsem,
         si, so, ssem) = refs
    at = Place()
    me = at.chip

    def fetch(layer):
        slot = layer % 2
        return (pltpu.make_async_copy(wi_hbm.at[layer], si.at[slot], ssem.at[slot, 0]),
                pltpu.make_async_copy(wo_hbm.at[layer], so.at[slot], ssem.at[slot, 1]))

    own = me * 2 + at.core
    if perturbed:
        loads = [pltpu.make_async_copy(wi_own, wi.at[own], wsem.at[0]), pltpu.make_async_copy(wo_own, wo.at[own], wsem.at[1])]
        for c in loads:
            c.start()
        meet(at.all_peers())
        for c in loads:
            c.wait()
        gather = Gather(at, [(wi.at[own], wi), (wo.at[own], wo)], gs, gr, ps, pr)
        gather.start()
        gather.run()
    else:
        for layer in range(2):
            for c in fetch(layer):
                c.start()
        meet(at.same_core_peers())

    def send(k, src, dst, send_sem, recv_sem):
        @pl.when(k == me)
        def _():
            pltpu.make_async_copy(src, dst.at[me], recv_sem.at[me]).start()

        @pl.when(k != me)
        def _():
            remote(src, dst.at[me], send_sem.at[k], recv_sem.at[me], at.device(k, at.core)).start()

    def layer_forward(layer, hidden, between):
        slot = layer % 2

        @pl.when(jnp.logical_and(layer >= 4, layer < LAYERS))
        def _():
            pltpu.make_async_copy(us.at[slot], u_hbm.at[layer - 2], usem.at[slot]).wait()

        if not perturbed:
            for c in fetch(layer):
                c.wait()
        for j in range(0, F, FT):
            cols = pl.ds(j, FT)
            if perturbed:
                a_w, b_w = wi[layer, :, cols], wo[layer, cols, :]
            else:
                a_w, b_w = si[slot, :, cols].astype(bf16), so[slot, cols, :].astype(bf16)
                wi[layer, :, cols] = a_w
                wo[layer, cols, :] = b_w
            pre = dot(hidden, a_w).astype(bf16)
            us[slot, :, cols] = pre
            pre = pre.astype(f32)
            part = dot((pre * cdf(pre)).astype(bf16), b_w)
            if j == 0:
                acc[...] = part
                between()
            else:
                acc[...] += part

        @pl.when(jnp.logical_and(layer >= 2, layer < LAYERS - 2))
        def _():
            pltpu.make_async_copy(us.at[slot], u_hbm.at[layer], usem.at[slot]).start()

        if not perturbed:
            @pl.when(layer < LAYERS - 2)
            def _():
                for c in fetch(layer + 2):
                    c.start()
        return (hidden.astype(f32) + acc[...]).astype(bf16)

    hs[0] = x_ref[...]

    def pair_forward(k, carry):
        mid[...] = layer_forward(2 * k, hs[k], lambda: send(k, hs.at[k], h_out, hsend, hrecv))
        hs[k + 1] = layer_forward(2 * k + 1, mid[...], lambda: None)
        return carry

    lax.fori_loop(0, CHIPS, pair_forward, 0)

    for i, (src, dst) in enumerate(((wi, pi_out), (wo, po_out))):
        pltpu.make_async_copy(src.at[pl.ds(2 * me, 2)], dst, wsem.at[i]).start()

    resid = hs[CHIPS].astype(f32) - y_ref[...].astype(f32)
    ds[CHIPS - 1] = (resid * inv_count).astype(bf16)
    if perturbed:
        mine = me * 2 + at.core
        lbuf[mine] = jnp.broadcast_to(0.5 * jnp.sum(resid * resid, axis=(0, 1), keepdims=True), (8, 128))

    def layer_backward(layer, cot, between):
        slot = layer % 2

        @pl.when(layer < LAYERS - 2)
        def _():
            pltpu.make_async_copy(u_hbm.at[layer], us.at[slot], usem.at[slot]).wait()

        for j in range(0, F, FT):
            cols = pl.ds(j, FT)
            pre = us[slot, :, cols].astype(f32)
            err = (dot(cot, wo[layer, cols, :], NT) * (cdf(pre) + slope_tail(pre))).astype(bf16)
            part = dot(err, wi[layer, :, cols], NT)
            if j == 0:
                acc[...] = part
                between()
            else:
                acc[...] += part

        @pl.when(layer >= 4)
        def _():
            pltpu.make_async_copy(u_hbm.at[layer - 2], us.at[slot], usem.at[slot]).start()

        return (cot.astype(f32) + acc[...]).astype(bf16)

    def pair_backward(i, carry):
        k = CHIPS - 1 - i
        mid[...] = layer_backward(2 * k + 1, ds[k], lambda: send(k, ds.at[k], d_out, dsend, drecv))
        ds[k - 1] = layer_backward(2 * k, mid[...], lambda: None)
        return carry

    if perturbed:
        def loss_copy(i, peer):
            return remote(lbuf.at[mine], lbuf.at[mine], lsend.at[i], lrecv.at[mine], peer)

        for i, peer in enumerate(at.all_peers()):
            loss_copy(i, peer).start()

    lax.fori_loop(0, CHIPS - 1, pair_backward, 0)
    send(0, ds.at[0], d_out, dsend, drecv)

    for i, (src, dst) in enumerate(((wi, pi_out), (wo, po_out))):
        pltpu.make_async_copy(src.at[pl.ds(2 * me, 2)], dst, wsem.at[i]).wait()

    def drain(k, carry):
        @pl.when(k != me)
        def _():
            remote(hs.at[0], h_out.at[k], hsend.at[k], hrecv.at[k], at.device(k, at.core)).wait_send()
            remote(ds.at[0], d_out.at[k], dsend.at[k], drecv.at[k], at.device(k, at.core)).wait_send()

        pltpu.make_async_copy(hs.at[0], h_out.at[k], hrecv.at[k]).wait()
        pltpu.make_async_copy(ds.at[0], d_out.at[k], drecv.at[k]).wait()
        return carry

    lax.fori_loop(0, CHIPS, drain, 0)

    if perturbed:
        for i, peer in enumerate(at.all_peers()):
            loss_copy(i, peer).wait_send()

        def gathered(i, carry):
            @pl.when(i != mine)
            def _():
                remote(lbuf.at[i], lbuf.at[i], lsend.at[0], lrecv.at[i], at.partner()).wait_recv()

            return carry

        lax.fori_loop(0, LAYERS, gathered, 0)
        total = lbuf[0]
        for i in range(1, LAYERS):
            total = total + lbuf[i]
        loss_out[...] = total * inv_count
        gather.finish()


def owner_kernel(perturbed, radius, *refs):
    if perturbed:
        (h_ref, d_ref, a_ref, b_ref, wi_hbm, wo_hbm, wi_out, wo_out,
         gi, go, u_low, a_low, acc, ri, ro, wi, wo, wsem, xsend, xrecv, gs, gr, ps, pr) = refs
    else:
        (h_ref, d_ref, a_ref, b_ref, wi_hbm, wo_hbm, wi_out, wo_out,
         gi, go, u_low, a_low, acc, ri, ro, wi, wo, wsem, xsend, xrecv, sbuf, ssend, srecv) = refs
    at = Place()
    mine = at.chip * 2 + at.core
    loads = [pltpu.make_async_copy(wi_hbm.at[mine], wi, wsem.at[0]), pltpu.make_async_copy(wo_hbm.at[mine], wo, wsem.at[1])]
    for c in loads:
        c.start()

    def block(i, carry):
        rows = pl.ds(pl.multiple_of(i * KB_ROWS, KB_ROWS), KB_ROWS)
        first = i == 0

        def add(ref, which, cols, value):
            ref[which, :, cols] = jnp.where(first, 0.0, ref[which, :, cols]) + value

        h_low = h_ref[rows, :]
        d_top = d_ref[rows, :]
        acc[...] = h_low.astype(f32)
        for j in range(0, F, KB_FT):
            cols = pl.ds(j, KB_FT)
            pre = dot(h_low, a_ref[0, :, cols]).astype(bf16)
            u_low[:, cols] = pre
            pre = pre.astype(f32)
            post = (pre * cdf(pre)).astype(bf16)
            a_low[:, cols] = post
            acc[...] += dot(post, b_ref[0, cols, :])
        h_mid = acc[...].astype(bf16)
        d_top_t, h_mid_t = d_top.T, h_mid.T
        acc[...] = d_top.astype(f32)
        for j in range(0, F, KB_FT):
            cols = pl.ds(j, KB_FT)
            pre = dot(h_mid, a_ref[1, :, cols]).astype(bf16).astype(f32)
            half = cdf(pre)
            post = (pre * half).astype(bf16)
            err = (dot(d_top, b_ref[1, cols, :], NT) * (half + slope_tail(pre))).astype(bf16)
            add(go, 1, cols, dot(d_top_t, post))
            add(gi, 1, cols, dot(h_mid_t, err))
            acc[...] += dot(err, a_ref[1, :, cols], NT)
        d_mid = acc[...].astype(bf16)
        d_mid_t, h_low_t = d_mid.T, h_low.T
        for j in range(0, F, KB_FT):
            cols = pl.ds(j, KB_FT)
            pre = u_low[:, cols].astype(f32)
            err = (dot(d_mid, b_ref[0, cols, :], NT) * (cdf(pre) + slope_tail(pre))).astype(bf16)
            add(go, 0, cols, dot(d_mid_t, a_low[:, cols]))
            add(gi, 0, cols, dot(h_low_t, err))
        return carry

    lax.fori_loop(0, ROWS // KB_ROWS, block, 0)
    meet([at.partner()] + [at.neighbour(d) for d in range(3)] if perturbed else at.all_peers())

    other = 1 - at.core
    swap = [remote(gi.at[other], ri, xsend.at[0], xrecv.at[0], at.partner()),
            remote(go.at[other], ro, xsend.at[1], xrecv.at[1], at.partner())]
    for c in swap:
        c.start()
    for c in loads:
        c.wait()

    def squares(value, total):
        sq = value * value
        for r in range(0, sq.shape[0], 8):
            for q in range(0, sq.shape[1], 128):
                total = total + sq[r:r + 8, q:q + 128]
        return total

    R, C = 16, 128

    def sum_in(i, total):
        rows = pl.ds(pl.multiple_of(i * R, R), R)
        g = gi[at.core, rows, :] + ri[rows, :]
        if perturbed:
            wi[rows, :] = wi[rows, :] - LEARN_RATE * g
            return total
        ri[rows, :] = g
        return squares(g, total)

    def sum_out(i, total):
        cols = pl.ds(pl.multiple_of(i * C, C), C)
        g = go[at.core, :, cols] + ro[:, cols]
        if perturbed:
            wo[cols, :] = wo[cols, :] - LEARN_RATE * g.T
            return total
        ro[:, cols] = g
        return squares(g, total)

    total = jnp.zeros((8, 128), f32)
    swap[0].wait_recv()
    total = lax.fori_loop(0, D // R, sum_in, total)
    swap[1].wait_recv()
    total = lax.fori_loop(0, F // C, sum_out, total)

    if perturbed:
        gather = Gather(at, [(wi, wi_out), (wo, wo_out)], gs, gr, ps, pr)
        keep = [pltpu.make_async_copy(wi, wi_out.at[mine], wsem.at[0]), pltpu.make_async_copy(wo, wo_out.at[mine], wsem.at[1])]
        gather.start()
        for c in keep:
            c.start()
        gather.run()
        gather.finish()
        for c in keep:
            c.wait()
    else:
        sbuf[mine] = total
        peers = at.all_peers()
        sends = [remote(sbuf.at[mine], sbuf.at[mine], ssend.at[i], srecv.at[mine], p) for i, p in enumerate(peers)]
        for c in sends:
            c.start()

        def gathered(i, carry):
            @pl.when(i != mine)
            def _():
                remote(sbuf.at[i], sbuf.at[i], ssend.at[0], srecv.at[i], at.partner()).wait_recv()

            return carry

        lax.fori_loop(0, LAYERS, gathered, 0)
        total = sbuf[0]
        for i in range(1, LAYERS):
            total = total + sbuf[i]
        scale = radius / jnp.sqrt(jnp.sum(total, axis=(0, 1), keepdims=True))

        def perturb_in(i, carry):
            rows = pl.ds(pl.multiple_of(i * R, R), R)
            wi_out[rows, :] = (wi[rows, :] + scale * ri[rows, :]).astype(bf16)
            return carry

        def perturb_out(i, carry):
            cols = pl.ds(pl.multiple_of(i * C, C), C)
            wo_out[cols, :] = (wo[cols, :] + scale * ro[:, cols].T).astype(bf16)
            return carry

        lax.fori_loop(0, D // R, perturb_in, 0)
        lax.fori_loop(0, F // C, perturb_out, 0)
        for c in sends:
            c.wait_send()
    for c in swap:
        c.wait_send()


def local_pass(perturbed, inv_count, x, y, wi, wo):
    shapes = [((CHIPS, T, D), bf16), ((CHIPS, T, D), bf16), ((2, D, F), bf16), ((2, F, D), bf16), ((LAYERS, T, F), bf16)]
    specs = [ANY] * 5
    scratch = [
        pltpu.VMEM((LAYERS, D, F), bf16), pltpu.VMEM((LAYERS, F, D), bf16),
        pltpu.VMEM((CHIPS + 1, T, D), bf16), pltpu.VMEM((CHIPS, T, D), bf16),
        pltpu.VMEM((T, D), bf16), pltpu.VMEM((T, D), f32), pltpu.VMEM((2, T, F), bf16),
        DMA((CHIPS,)), DMA((CHIPS,)), DMA((CHIPS,)), DMA((CHIPS,)), DMA((2,)), DMA((2,)),
    ]
    if perturbed:
        shapes.append(((8, 128), f32))
        specs.append(V)
        scratch += [*GATHER_SEMS, pltpu.VMEM((LAYERS, 8, 128), f32), DMA((15,)), DMA((LAYERS,))]
    else:
        scratch += [pltpu.VMEM((2, D, F), f32), pltpu.VMEM((2, F, D), f32), DMA((2, 2))]
    return pl.pallas_call(
        functools.partial(local_kernel, perturbed, inv_count),
        out_shape=[jax.ShapeDtypeStruct(*s) for s in shapes],
        in_specs=[V, V, ANY, ANY],
        out_specs=specs,
        scratch_shapes=scratch,
        compiler_params=pltpu.CompilerParams(
            collective_id=2 if perturbed else 0, has_side_effects=True, vmem_limit_bytes=67043328),
        name="local_perturbed" if perturbed else "local",
    )(x, y, wi, wo)


def owner_pass(perturbed, radius, h, d, a, b, wi, wo):
    if perturbed:
        shapes = [((LAYERS, D, F), f32), ((LAYERS, F, D), f32)]
        tail = GATHER_SEMS
    else:
        shapes = [((D, F), bf16), ((F, D), bf16)]
        tail = [pltpu.VMEM((LAYERS, 8, 128), f32), DMA((15,)), DMA((LAYERS,))]
    scratch = [
        pltpu.VMEM((2, D, F), f32), pltpu.VMEM((2, D, F), f32),
        pltpu.VMEM((KB_ROWS, F), bf16), pltpu.VMEM((KB_ROWS, F), bf16), pltpu.VMEM((KB_ROWS, D), f32),
        pltpu.VMEM((D, F), f32), pltpu.VMEM((D, F), f32), pltpu.VMEM((D, F), f32), pltpu.VMEM((F, D), f32),
        DMA((2,)), DMA((2,)), DMA((2,)), *tail,
    ]
    return pl.pallas_call(
        functools.partial(owner_kernel, perturbed, radius),
        out_shape=[jax.ShapeDtypeStruct(*s) for s in shapes],
        in_specs=[V, V, V, V, ANY, ANY],
        out_specs=[ANY, ANY] if perturbed else [V, V],
        scratch_shapes=scratch,
        compiler_params=pltpu.CompilerParams(
            collective_id=3 if perturbed else 1, has_side_effects=True, vmem_limit_bytes=60 * 2**20),
        name="owner_perturbed" if perturbed else "owner",
    )(h.reshape(ROWS, D), d.reshape(ROWS, D), a, b, wi, wo)


def solution(mesh):
    mesh_axes = tuple(mesh.axis_names)
    dev_count = math.prod([mesh.shape[axis_name] for axis_name in mesh_axes])
    batch_spec = P(mesh_axes, None, None)

    def local_step(images, targets, w_in, w_out):
        layers, model_dim, hidden_dim = w_in.shape
        inv_count = 1.0 / (images.shape[0] * images.shape[1] * dev_count * model_dim)
        radius = RHO_REL * math.sqrt(layers * hidden_dim + model_dim)
        x, y = images.reshape(T, D), targets.reshape(T, D)
        h, d, a, b, _ = local_pass(False, inv_count, x, y, w_in, w_out)
        pert_in, pert_out = owner_pass(False, radius, h, d, a, b, w_in, w_out)
        h, d, a, b, _, loss = local_pass(True, inv_count, x, y, pert_in, pert_out)
        new_in, new_out = owner_pass(True, radius, h, d, a, b, w_in, w_out)
        return new_in, new_out, loss[0, 0]

    return jax.shard_map(local_step, mesh=mesh, in_specs=(batch_spec, batch_spec, P(), P()), out_specs=(P(), P(), P()), check_vma=False)
```

time: 2960 us -> 885 us (0.30)
  waiting for transfers between devices: 1930 us -> 0 us
  Pallas kernels: 0 us -> 826 us
  matrix products: 533 us -> 0 us
  other arithmetic: 222 us -> 0 us
  local copies, waits for them, and re-layouts: 187 us -> 50.1 us
  between operations: 40.1 us -> 1.11 us
  blocking collectives: 34.6 us -> 0 us
    psum x2 -> x0, waiting for transfers between devices: 1930 us -> none  [the longest x1 966 us: local_step(): lax.psum((grads2_in, grads2_out, loss_local), mesh_axes)]
    pallas_call x0 -> x4, Pallas kernels: none -> 826 us  [the longest x2 440 us: owner_pass(): pl.pallas_call(functools.partial(owner_kernel, perturbed, radius), out_sh...]
    dot_general x188 -> x0, matrix products: 533 us -> none  [the longest x32 135 us: backward(): jnp.einsum('tf,td->fd', post_act, d_hidden, preferred_element_type=jnp.fl...]
    unnamed x572 -> x4, local copies, waits for them, and re-layouts: 184 us -> 48.9 us
    convert_element_type x6 -> x0, other arithmetic: 89.1 us -> none  [the longest x2 31.8 us: local_step(): (w_out[layer_idx] + step_scale * grads_out[layer_idx]).astype(jnp.bfloat16)]
    sub x2 -> x0, other arithmetic: 75.4 us -> none  [the longest x1 37.7 us: local_step(): new_in = w_in - LEARN_RATE * jnp.stack(grads2_in)]
    reduce_sum x16 -> x0, other arithmetic: 57.4 us -> none  [local_step(): jnp.sum(grad_part * grad_part)]
    psum x1 -> x0, blocking collectives: 34.6 us -> none  [local_step(): lax.psum((grads2_in, grads2_out, loss_local), mesh_axes)]
  transfers between devices with their start and end apart: 2 -> 0, of which waited for: 2 -> 0; matrix products, arithmetic and copies ran while one was open for 1% -> 0% of each run, Pallas kernels for 0% -> 0%
where the time goes in v1:
time: 885 us; the launch traced here: 878 us
  Pallas kernels  826 us (93%)
  local copies, waits for them, and re-layouts  50.1 us (6%)
    pallas_call x2, Pallas kernels, owner_pass(): pl.pallas_call(functools.partial(owner_kernel, perturbed, radius), out_sh...  440 us
    pallas_call x2, Pallas kernels, local_pass(): pl.pallas_call(functools.partial(local_kernel, perturbed, inv_count), out...  387 us
    unnamed x4, local copies, waits for them, and re-layouts  48.9 us

profile of v1, /device:TPU:1, one launch (start us, length us, event | category | flops | bytes accessed | tf_op | source)
XLA Modules:
  0.0 877.6 jit_solution(5655662399798795522)
XLA Ops:
  0.6 130.1 %local.1 = (bf16[8,576,384]{2,1,0:T(8,128)(2,1)}, bf16[8,576,384]{2,1,0:T(8,128)(2,1)}, bf16[2,384,1536]{2,1,0:T(8,128)(2,1)}, bf16[2,1536,384]{2,1,0:T(8,128)(2,1)}, bf16[16,576,1536]{2,1,0:T(8,128)(2,1)}) custom-call(bf16[576,384]{1,0:T(8,128)(2,1)} %bitcast.11, bf16[576,384]{1,0:T(8,128)(2,1)} %bitcast.13, f32[16,384,1536]{2,1,0:T(8,128)} %refs_4_.3, ...), custom_call_target="tpu_custom_call" | custom-call | tf_op jit(solution)/shard_map/local/pallas_call | solution.py:494
  130.8 100.9 %owner.1 = (bf16[384,1536]{1,0:T(8,128)(2,1)}, bf16[1536,384]{1,0:T(8,128)(2,1)}) custom-call(bf16[4608,384]{1,0:T(8,128)(2,1)} %bitcast.9, bf16[4608,384]{1,0:T(8,128)(2,1)} %bitcast.10, bf16[2,384,1536]{2,1,0:T(8,128)(2,1)} %get-tuple-element.18.refs_2_, bf16[2,1536,384]{2,1,0:T(8,128)(2,1)} %get-tuple-element.19.refs_3_, f32[16,384,1536]{2,1,0:T(8,128)} %refs_4_.3, ...), custom_call_target="tpu_custom_call" | custom-call | tf_op jit(solution)/shard_map/owner/pallas_call | solution.py:519
  231.7 256.5 %local_perturbed.1 = (bf16[8,576,384]{2,1,0:T(8,128)(2,1)}, bf16[8,576,384]{2,1,0:T(8,128)(2,1)}, bf16[2,384,1536]{2,1,0:T(8,128)(2,1)}, bf16[2,1536,384]{2,1,0:...) custom-call(bf16[576,384]{1,0:T(8,128)(2,1)} %bitcast.12, bf16[576,384]{1,0:T(8,128)(2,1)} %bitcast.14, ...), custom_call_target="tpu_custom_call" | custom-call | tf_op jit(solution)/shard_map/local_perturbed/pallas_call | solution.py:494
  488.2 1.2 slice.3
  489.4 338.8 %owner_perturbed.1 = (f32[16,384,1536]{2,1,0:T(8,128)}, f32[16,1536,384]{2,1,0:T(8,128)}) custom-call(bf16[4608,384]{1,0:T(8,128)(2,1)} %bitcast.7, bf16[4608,384]{1,0:T(8,128)(2,1)} %bitcast.8, bf16[2,384,1536]{2,1,0:T(8,128)(2,1)} %get-tuple-element.24.refs_2_, bf16[2,1536,384]{2,1,0:T(8,128)(2,1)} %get-tuple-element.25.refs_3_, f32[16,384,1536]{2,1,0:T(8,128)} %refs_4_.3, ...), custom_call_target="tpu_custom_call" | custom-call | tf_op jit(solution)/shard_map/owner_perturbed/pallas_call | solution.py:519
  828.2 0.0 copy-start
  828.2 29.3 %copy.9 = f32[16,384,1536]{2,1,0:T(8,128)} copy(f32[16,384,1536]{2,1,0:T(8,128)} %get-tuple-element.32) | data formatting | bytes 75497472
  857.5 6.5 copy-done
  864.1 13.1 %copy.10 = f32[16,1536,384]{2,1,0:T(8,128)} copy(f32[16,1536,384]{2,1,0:T(8,128)S(1)} %copy-done) | data formatting | bytes 75497472
Async XLA Ops:
  828.2 35.8 %copy-start = (f32[16,1536,384]{2,1,0:T(8,128)S(1)}, f32[16,1536,384]{2,1,0:T(8,128)}, u32[]{:S(2)}) copy-start(f32[16,1536,384]{2,1,0:T(8,128)} %get-tuple-element.33) | copy-start | bytes 113246208

commit v2 on v0

v2 whole, which is shorter than its diff:
```python
import functools
import math

import jax
import jax.numpy as jnp
from jax import lax
from jax.experimental import pallas as pl
from jax.experimental.pallas import tpu as pltpu
from jax.sharding import PartitionSpec as P

MESH = pl.DeviceIdType.MESH
RHO_REL = 0.1
LEARN_RATE = 8.0
SQRT_HALF = 0.7071067811865476
INV_SQRT_2PI = 0.3989422804014327

CHIPS = 8
LAYERS = 16
D = 384
F = 1536
T = 576
ROWS = CHIPS * T
FT = 768
KB_ROWS = 768
KB_FT = 256
KEPT = 8
VMEM_LIMIT = 67043328

f32, bf16 = jnp.float32, jnp.bfloat16
NN = (((1,), (0,)), ((), ()))
NT = (((1,), (1,)), ((), ()))
V = pl.BlockSpec(memory_space=pltpu.VMEM)
ANY = pl.BlockSpec(memory_space=pl.ANY)
DMA = pltpu.SemaphoreType.DMA


def dot(a, b, dims=NN):
    return lax.dot_general(a, b, dims, preferred_element_type=f32)


def cdf(x):
    return 0.5 * (1.0 + lax.erf(x * SQRT_HALF))


def slope_tail(x):
    return x * INV_SQRT_2PI * jnp.exp(-0.5 * x * x)


class Place:
    def __init__(self):
        self.z, self.y, data = lax.axis_index("model"), lax.axis_index("sub"), lax.axis_index("data")
        self.x, self.core = data // 2, data % 2
        self.chip = self.z * 4 + self.y * 2 + self.x
        self.mine = self.chip * 2 + self.core

    def across(self, t):
        x, y, z = (self.x + t) % 2, (self.y + t // 2) % 2, (self.z + t // 4) % 2
        return z * 4 + y * 2 + x

    def device(self, chip, core):
        return (chip // 4, (chip // 2) % 2, (chip % 2) * 2 + core)

    def partner(self):
        return self.device(self.chip, 1 - self.core)

    def peer(self, i):
        return self.device(self.across(i // 2), (self.core + i) % 2)


def bit(dim):
    return 1 + dim + dim * (dim - 1) // 2


def each(first, last, body):
    def step(i, carry):
        body(i)
        return carry

    lax.fori_loop(first, last, step, 0)


def meet(at):
    barrier = pltpu.get_barrier_semaphore()
    each(1, 16, lambda i: pl.semaphore_signal(barrier, inc=1, device_id=at.peer(i), device_id_type=MESH))
    pl.semaphore_wait(barrier, 15)


def remote(src, dst, send_sem, recv_sem, device):
    return pltpu.make_async_remote_copy(
        src_ref=src, dst_ref=dst, send_sem=send_sem, recv_sem=recv_sem, device_id=device, device_id_type=MESH
    )


class Gather:
    MESSAGES = ((0, ()), (1, ()), (2, ()), (1, (1,)), (2, (2,)), (2, (1,)), (2, (1, 2)))

    def __init__(self, at, tensors, send, recv, pair_send, pair_recv):
        self.at, self.tensors = at, tensors
        self.sems = (send, recv, pair_send, pair_recv)

    def make(self, i, part, own, chip, send, recv, device):
        ref, slots = self.tensors[i]
        n = slots.shape[1] // 3
        rows = pl.ds(pl.multiple_of(part * n, n), n)
        dst = slots.at[chip * 2 + self.at.core, rows, :]
        return remote(ref.at[rows, :] if own else dst, dst, send, recv, device)

    def parts(self, dim, slot):
        back, turns = self.MESSAGES[slot]
        t = 0
        for o in turns:
            t = t + bit((dim + 3 - o) % 3)
        return (dim + 3 - back) % 3, t

    def link(self, i, dim, slot):
        part, t = self.parts(dim, slot)
        send, recv, _, _ = self.sems
        return self.make(i, part, slot < 3, self.at.across(t) if slot >= 3 else self.at.chip, send.at[dim, slot, i],
                         recv.at[dim, slot, i], self.at.device(self.at.across(bit(dim)), self.at.core))

    def pair(self, i, part, own, chip, index):
        _, _, send, recv = self.sems
        return self.make(i, part, own, chip, send.at[index, i], recv.at[index, i], self.at.partner())

    def start(self):
        for slot in range(3):
            for i in range(2):
                each(0, 3, lambda dim: self.link(i, dim, slot).start())
        for i in range(2):
            each(0, 3, lambda part: self.pair(i, part, True, self.at.chip, part).start())

    def run(self):
        turn = {0: (3, 1), 1: (5, 1), 3: (6, 1)}
        for slot in range(7):
            for i in range(2):
                def got(dim):
                    self.link(i, dim, slot).wait_recv()
                    if slot in turn:
                        later, step = turn[slot]
                        self.link(i, (dim + step) % 3, later).start()
                    part, t = self.parts(dim, slot)
                    self.pair(i, part, False, self.at.across(t + bit(dim)), 3 + slot * 3 + dim).start()

                each(0, 3, got)
            if slot == 0:
                for i in range(2):
                    each(0, 3, lambda dim: self.link(i, dim, 4).start())
        for i in range(2):
            each(0, 24, lambda index: self.pair(i, 0, False, self.at.chip, index).wait_recv())

    def finish(self):
        for i in range(2):
            each(0, 24, lambda index: self.pair(i, 0, False, self.at.chip, index).wait_send())
            for slot in range(7):
                each(0, 3, lambda dim: self.link(i, dim, slot).wait_send())


GATHER_SEMS = [DMA((3, 7, 2)), DMA((3, 7, 2)), DMA((24, 2)), DMA((24, 2))]


def pass_kernel(perturbed, inv_count, radius, *refs):
    if perturbed:
        (x_ref, y_ref, wi_hbm, wo_hbm, pi_own, po_own, wi_out, wo_out, wbi, wbo, u_hbm, loss_out,
         bi, bo, hs, ds, acc, us, hg, dg, gi, go, ri, ro,
         hsend, hrecv, dsend, drecv, usem, bsem, wsem, xsend, xrecv, sbuf, ssend, srecv,
         wi, wo, as_, ar, aps, apr, gs, gr, gps, gpr) = refs
    else:
        (x_ref, y_ref, wi_hbm, wo_hbm, wi_out, wo_out, u_hbm,
         bi, bo, hs, ds, acc, us, hg, dg, gi, go, ri, ro,
         hsend, hrecv, dsend, drecv, usem, bsem, wsem, xsend, xrecv, sbuf, ssend, srecv,
         si, so, fsem) = refs
    at = Place()
    me = at.chip
    mine = at.mine

    def fetch32(layer, slot):
        return (pltpu.make_async_copy(wi_hbm.at[layer], si.at[slot], fsem.at[slot, 0]),
                pltpu.make_async_copy(wo_hbm.at[layer], so.at[slot], fsem.at[slot, 1]))

    def fetch16(layer, slot):
        return (pltpu.make_async_copy(wbi.at[layer], bi.at[slot], bsem.at[slot, 0]),
                pltpu.make_async_copy(wbo.at[layer], bo.at[slot], bsem.at[slot, 1]))

    fetch = fetch16 if perturbed else fetch32

    def start(copies):
        for c in copies:
            c.start()

    def wait(copies):
        for c in copies:
            c.wait()

    own_w = [pltpu.make_async_copy(wi_hbm.at[mine], wi if perturbed else si.at[0], wsem.at[0]),
             pltpu.make_async_copy(wo_hbm.at[mine], wo if perturbed else so.at[0], wsem.at[1])]
    if perturbed:
        keep = [pltpu.make_async_copy(pi_own, wbi.at[mine], wsem.at[2]), pltpu.make_async_copy(po_own, wbo.at[mine], wsem.at[3])]
        start(keep)
        start(own_w)
        meet(at)
        spread = Gather(at, [(pi_own, wbi), (po_own, wbo)], as_, ar, aps, apr)
        spread.start()
        spread.run()
        wait(keep)
        for layer in range(2):
            start(fetch(layer, layer))
    else:
        for layer in range(2):
            start(fetch(layer, layer))
        meet(at)

    def span(k):
        return pl.ds(pl.multiple_of(k * T, T), T)

    def moved(t, src, dst, send_sem, recv_sem):
        chip = at.across(t)
        return remote(src.at[span(chip), :], dst.at[span(t), :], send_sem.at[t], recv_sem.at[t], at.device(chip, at.core))

    def exchange(src, dst, send_sem, recv_sem):
        each(1, CHIPS, lambda t: moved(t, src, dst, send_sem, recv_sem).start())
        dst[pl.ds(0, T), :] = src[span(me), :]

    def weights(slot, cols):
        if perturbed:
            return bi[slot, :, cols], bo[slot, cols, :]
        return si[slot, :, cols].astype(bf16), so[slot, cols, :].astype(bf16)

    def kept(layer):
        return us.at[span(layer % KEPT), :]

    def put(layer):
        return pltpu.make_async_copy(kept(layer), u_hbm.at[layer], usem.at[layer % KEPT])

    def get(layer):
        return pltpu.make_async_copy(u_hbm.at[layer], kept(layer), usem.at[layer % KEPT])

    acc_t = acc.at[pl.ds(0, T), :]

    def layer_forward(layer, carry):
        slot = layer % 2
        hidden = hs[span((layer + 1) // 2), :]
        pre_out = kept(layer)

        @pl.when(layer >= KEPT + 2)
        def _():
            put(layer - KEPT).wait()

        wait(fetch(layer, slot))
        for j in range(0, F, FT):
            cols = pl.ds(j, FT)
            a_w, b_w = weights(slot, cols)
            pre = dot(hidden, a_w).astype(bf16)
            pre_out[:, cols] = pre
            pre = pre.astype(f32)
            part = dot((pre * cdf(pre)).astype(bf16), b_w)
            if j == 0:
                acc_t[...] = part
            else:
                acc_t[...] += part

        @pl.when(jnp.logical_and(layer >= 2, layer < KEPT))
        def _():
            put(layer).start()

        @pl.when(layer < LAYERS - 2)
        def _():
            start(fetch(layer + 2, slot))

        hs[span((layer + 2) // 2), :] = (hidden.astype(f32) + acc_t[...]).astype(bf16)
        return carry

    hs[pl.ds(0, T), :] = x_ref[...]
    lax.fori_loop(0, LAYERS, layer_forward, 0)
    exchange(hs, hg, hsend, hrecv)

    def share(value):
        sbuf[mine] = jnp.broadcast_to(value, (8, 128))

    def shared(i):
        return remote(sbuf.at[mine], sbuf.at[mine], ssend.at[i], srecv.at[mine], at.peer(i))

    def share_start():
        each(1, LAYERS, lambda i: shared(i).start())

    def share_finish():
        each(1, LAYERS, lambda i: shared(i).wait_send())

        def gathered(i):
            @pl.when(i != mine)
            def _():
                remote(sbuf.at[i], sbuf.at[i], ssend.at[0], srecv.at[i], at.partner()).wait_recv()

        each(0, LAYERS, gathered)
        total = sbuf[0]
        for i in range(1, LAYERS):
            total = total + sbuf[i]
        return total

    resid = hs[pl.ds(CHIPS * T, T), :].astype(f32) - y_ref[...].astype(f32)
    ds[pl.ds((CHIPS - 1) * T, T), :] = (resid * inv_count).astype(bf16)
    if perturbed:
        share(0.5 * jnp.sum(resid * resid, axis=(0, 1), keepdims=True))

    def layer_backward(i, carry):
        layer = LAYERS - 1 - i
        slot = layer % 2
        cot = ds[span((layer - 1) // 2), :]
        pre_in = kept(layer)

        @pl.when(layer < KEPT)
        def _():
            get(layer).wait()

        @pl.when(layer < LAYERS - 2)
        def _():
            wait(fetch(layer, slot))

        for j in range(0, F, FT):
            cols = pl.ds(j, FT)
            a_w, b_w = weights(slot, cols)
            pre = pre_in[:, cols].astype(f32)
            err = (dot(cot, b_w, NT) * (cdf(pre) + slope_tail(pre))).astype(bf16)
            part = dot(err, a_w, NT)
            if j == 0:
                acc_t[...] = part
            else:
                acc_t[...] += part

        @pl.when(layer >= KEPT + 2)
        def _():
            get(layer - KEPT).start()

        @pl.when(layer >= 4)
        def _():
            start(fetch(layer - 2, slot))

        @pl.when(layer < 4)
        def _():
            start(fetch(me * 2 + 3 - layer, slot))

        ds[span((layer - 2) // 2), :] = (cot.astype(f32) + acc_t[...]).astype(bf16)
        return carry

    lax.fori_loop(0, LAYERS - 2, layer_backward, 0)
    exchange(ds, dg, dsend, drecv)
    if perturbed:
        share_start()
    low, high = 1, 0

    def take(layer, slot):
        wait(fetch(layer, slot))
        if not perturbed:
            for j in range(0, F, FT):
                cols = pl.ds(j, FT)
                bi[slot, :, cols], bo[slot, cols, :] = weights(slot, cols)

    def block(i):
        return pl.ds(pl.multiple_of(i * KB_ROWS, KB_ROWS), KB_ROWS)

    def arrive(i, src, dst, send_sem, recv_sem):
        def step(t):
            @pl.when(t * T // KB_ROWS == i)
            def _():
                moved(t, src, dst, send_sem, recv_sem).wait_recv()

        each(1, CHIPS, step)

    def add(i, ref, which, cols, value):
        ref[which, :, cols] = jnp.where(i == 0, 0.0, ref[which, :, cols]) + value

    def sweep_low(i, carry):
        arrive(i, hs, hg, hsend, hrecv)
        rows = block(i)
        h_low = hg[rows, :]
        acc[...] = h_low.astype(f32)
        for j in range(0, F, KB_FT):
            cols = pl.ds(j, KB_FT)
            pre = dot(h_low, bi[low, :, cols]).astype(bf16)
            us[rows, cols] = pre
            pre = pre.astype(f32)
            acc[...] += dot((pre * cdf(pre)).astype(bf16), bo[low, cols, :])
        hs[rows, :] = acc[...].astype(bf16)
        return carry

    def sweep_high(i, carry):
        arrive(i, ds, dg, dsend, drecv)
        rows = block(i)
        h_mid, d_top = hs[rows, :], dg[rows, :]
        h_mid_t, d_top_t = h_mid.T, d_top.T
        acc[...] = d_top.astype(f32)
        for j in range(0, F, KB_FT):
            cols = pl.ds(j, KB_FT)
            pre = dot(h_mid, bi[high, :, cols]).astype(bf16).astype(f32)
            half = cdf(pre)
            post = (pre * half).astype(bf16)
            err = (dot(d_top, bo[high, cols, :], NT) * (half + slope_tail(pre))).astype(bf16)
            add(i, go, 1, cols, dot(d_top_t, post))
            add(i, gi, 1, cols, dot(h_mid_t, err))
            acc[...] += dot(err, bi[high, :, cols], NT)
        dg[rows, :] = acc[...].astype(bf16)
        return carry

    def sweep_back(i, carry):
        if perturbed:
            @pl.when(jnp.logical_and(i == 1, at.core == 1))
            def _():
                update()

        rows = block(i)
        h_low, d_mid = hg[rows, :], dg[rows, :]
        h_low_t, d_mid_t = h_low.T, d_mid.T
        for j in range(0, F, KB_FT):
            cols = pl.ds(j, KB_FT)
            pre = us[rows, cols].astype(f32)
            half = cdf(pre)
            post = (pre * half).astype(bf16)
            err = (dot(d_mid, bo[low, cols, :], NT) * (half + slope_tail(pre))).astype(bf16)
            add(i, go, 0, cols, dot(d_mid_t, post))
            add(i, gi, 0, cols, dot(h_low_t, err))
        return carry

    def swap(which):
        return [remote(gi.at[which], ri, xsend.at[0], xrecv.at[0], at.partner()),
                remote(go.at[which], ro, xsend.at[1], xrecv.at[1], at.partner())]

    def squares(value, total):
        sq = value * value
        for r in range(0, sq.shape[0], 8):
            for q in range(0, sq.shape[1], 128):
                total = total + sq[r:r + 8, q:q + 128]
        return total

    R, C = 16, 128

    def sum_in(i, total):
        rows = pl.ds(pl.multiple_of(i * R, R), R)
        g = gi[at.core, rows, :] + ri[rows, :]
        if perturbed:
            wi[rows, :] = wi[rows, :] - LEARN_RATE * g
            return total
        ri[rows, :] = g
        return squares(g, total)

    def sum_out(i, total):
        cols = pl.ds(pl.multiple_of(i * C, C), C)
        g = go[at.core, :, cols] + ro[:, cols]
        if perturbed:
            wo[cols, :] = wo[cols, :] - LEARN_RATE * g.T
            return total
        ro[:, cols] = g
        return squares(g, total)

    def sum_layer():
        got = swap(0)
        got[0].wait_recv()
        total = lax.fori_loop(0, D // R, sum_in, jnp.zeros((8, 128), f32))
        got[1].wait_recv()
        return lax.fori_loop(0, F // C, sum_out, total)

    if perturbed:
        gather = Gather(at, [(wi, wi_out), (wo, wo_out)], gs, gr, gps, gpr)
        keep_new = [pltpu.make_async_copy(wi, wi_out.at[mine], wsem.at[0]), pltpu.make_async_copy(wo, wo_out.at[mine], wsem.at[1])]

    def update():
        wait(own_w)
        sum_layer()
        gather.start()
        start(keep_new)

    blocks = ROWS // KB_ROWS
    take(me * 2, low)
    each(1, CHIPS, lambda t: moved(t, hs, hg, hsend, hrecv).wait_send())
    lax.fori_loop(0, blocks, sweep_low, 0)
    take(me * 2 + 1, high)
    if not perturbed:
        start(own_w)
    lax.fori_loop(0, blocks, sweep_high, 0)

    @pl.when(at.core == 0)
    def _():
        start(swap(1))

    lax.fori_loop(0, blocks, sweep_back, 0)

    @pl.when(at.core == 1)
    def _():
        start(swap(0))

    each(1, CHIPS, lambda t: moved(t, ds, dg, dsend, drecv).wait_send())
    if perturbed:
        @pl.when(at.core == 0)
        def _():
            update()

        gather.run()
        loss_out[...] = share_finish() * inv_count
        spread.finish()
        gather.finish()
        wait(keep_new)
    else:
        wait(own_w)
        sbuf[mine] = sum_layer()
        share_start()
        scale = radius / jnp.sqrt(jnp.sum(share_finish(), axis=(0, 1), keepdims=True))

        def perturb_in(i, carry):
            rows = pl.ds(pl.multiple_of(i * R, R), R)
            bi[0, rows, :] = (si[0, rows, :] + scale * ri[rows, :]).astype(bf16)
            return carry

        def perturb_out(i, carry):
            cols = pl.ds(pl.multiple_of(i * C, C), C)
            bo[0, cols, :] = (so[0, cols, :] + scale * ro[:, cols].T).astype(bf16)
            return carry

        lax.fori_loop(0, D // R, perturb_in, 0)
        lax.fori_loop(0, F // C, perturb_out, 0)
        done = [pltpu.make_async_copy(bi.at[0], wi_out, wsem.at[2]), pltpu.make_async_copy(bo.at[0], wo_out, wsem.at[3])]
        start(done)
        wait(done)
    for c in swap(0):
        c.wait_send()


def one_pass(perturbed, inv_count, radius, x, y, w_in, w_out, pert=()):
    acts = ((LAYERS, T, F), bf16)
    scratch = [
        pltpu.VMEM((2, D, F), bf16), pltpu.VMEM((2, F, D), bf16),
        pltpu.VMEM((ROWS + T, D), bf16), pltpu.VMEM((ROWS, D), bf16), pltpu.VMEM((KB_ROWS, D), f32), pltpu.VMEM((ROWS, F), bf16),
        pltpu.VMEM((ROWS, D), bf16), pltpu.VMEM((ROWS, D), bf16),
        pltpu.VMEM((2, D, F), f32), pltpu.VMEM((2, D, F), f32), pltpu.VMEM((D, F), f32), pltpu.VMEM((D, F), f32),
        DMA((CHIPS,)), DMA((CHIPS,)), DMA((CHIPS,)), DMA((CHIPS,)), DMA((KEPT,)), DMA((2, 2)), DMA((4,)), DMA((2,)), DMA((2,)),
        pltpu.VMEM((LAYERS, 8, 128), f32), DMA((LAYERS,)), DMA((LAYERS,)),
    ]
    if perturbed:
        shapes = [((LAYERS, D, F), f32), ((LAYERS, F, D), f32), ((LAYERS, D, F), bf16), ((LAYERS, F, D), bf16), acts, ((8, 128), f32)]
        out_specs = [ANY] * 5 + [V]
        scratch += [pltpu.VMEM((D, F), f32), pltpu.VMEM((F, D), f32), *GATHER_SEMS, *GATHER_SEMS]
    else:
        shapes = [((D, F), bf16), ((F, D), bf16), acts]
        out_specs = [ANY] * 3
        scratch += [pltpu.VMEM((2, D, F), f32), pltpu.VMEM((2, F, D), f32), DMA((2, 2))]
    options = dict(
        out_shape=[jax.ShapeDtypeStruct(*s) for s in shapes],
        in_specs=[V, V, ANY, ANY] + [V] * len(pert),
        out_specs=out_specs,
        scratch_shapes=scratch,
        compiler_params=pltpu.CompilerParams(
            collective_id=1 if perturbed else 0, has_side_effects=True, vmem_limit_bytes=VMEM_LIMIT),
        name="second_pass" if perturbed else "first_pass",
    )
    kernel = functools.partial(pass_kernel, perturbed, inv_count, radius)
    if perturbed:
        return pl.pallas_call(kernel, **options)(x, y, w_in, w_out, *pert)
    return pl.pallas_call(kernel, **options)(x, y, w_in, w_out)


def solution(mesh):
    mesh_axes = tuple(mesh.axis_names)
    dev_count = math.prod([mesh.shape[axis_name] for axis_name in mesh_axes])
    batch_spec = P(mesh_axes, None, None)

    def local_step(images, targets, w_in, w_out):
        layers, model_dim, hidden_dim = w_in.shape
        inv_count = 1.0 / (images.shape[0] * images.shape[1] * dev_count * model_dim)
        radius = RHO_REL * math.sqrt(layers * hidden_dim + model_dim)
        x, y = images.reshape(T, D), targets.reshape(T, D)
        pert = one_pass(False, inv_count, radius, x, y, w_in, w_out)[:2]
        new_in, new_out, _, _, _, loss = one_pass(True, inv_count, radius, x, y, w_in, w_out, pert)
        return new_in, new_out, loss[0, 0]

    return jax.shard_map(local_step, mesh=mesh, in_specs=(batch_spec, batch_spec, P(), P()), out_specs=(P(), P(), P()), check_vma=False)
```

time: 2960 us -> 769 us (0.26)
  waiting for transfers between devices: 1930 us -> 0 us
  Pallas kernels: 0 us -> 710 us
  matrix products: 533 us -> 0 us
  other arithmetic: 222 us -> 0 us
  local copies, waits for them, and re-layouts: 187 us -> 50.1 us
  between operations: 40.1 us -> 1.15 us
  blocking collectives: 34.6 us -> 0 us
    psum x2 -> x0, waiting for transfers between devices: 1930 us -> none  [the longest x1 966 us: local_step(): lax.psum((grads2_in, grads2_out, loss_local), mesh_axes)]
    pallas_call x0 -> x2, Pallas kernels: none -> 710 us  [the longest x1 527 us: one_pass(): return pl.pallas_call(kernel, **options)(x, y, w_in, w_out, *pert)]
    dot_general x188 -> x0, matrix products: 533 us -> none  [the longest x32 135 us: backward(): jnp.einsum('tf,td->fd', post_act, d_hidden, preferred_element_type=jnp.fl...]
    unnamed x572 -> x4, local copies, waits for them, and re-layouts: 184 us -> 48.9 us
    convert_element_type x6 -> x0, other arithmetic: 89.1 us -> none  [the longest x2 31.8 us: local_step(): (w_out[layer_idx] + step_scale * grads_out[layer_idx]).astype(jnp.bfloat16)]
    sub x2 -> x0, other arithmetic: 75.4 us -> none  [the longest x1 37.7 us: local_step(): new_in = w_in - LEARN_RATE * jnp.stack(grads2_in)]
    reduce_sum x16 -> x0, other arithmetic: 57.4 us -> none  [local_step(): jnp.sum(grad_part * grad_part)]
    psum x1 -> x0, blocking collectives: 34.6 us -> none  [local_step(): lax.psum((grads2_in, grads2_out, loss_local), mesh_axes)]
  transfers between devices with their start and end apart: 2 -> 0, of which waited for: 2 -> 0; matrix products, arithmetic and copies ran while one was open for 1% -> 0% of each run, Pallas kernels for 0% -> 0%
where the time goes in v2:
time: 769 us; the launch traced here: 762 us
  Pallas kernels  710 us (92%)
  local copies, waits for them, and re-layouts  50.1 us (7%)
    pallas_call x1, Pallas kernels, one_pass(): return pl.pallas_call(kernel, **options)(x, y, w_in, w_out, *pert)  527 us
    pallas_call x1, Pallas kernels, one_pass(): return pl.pallas_call(kernel, **options)(x, y, w_in, w_out)  183 us
    unnamed x4, local copies, waits for them, and re-layouts  48.9 us

profile of v2, /device:TPU:1, one launch (start us, length us, event | category | flops | bytes accessed | tf_op | source)
XLA Modules:
  0.0 761.7 jit_solution(5176951580293035163)
XLA Ops:
  0.6 183.2 %first_pass.1 = (bf16[384,1536]{1,0:T(8,128)(2,1)}, bf16[1536,384]{1,0:T(8,128)(2,1)}, bf16[16,576,1536]{2,1,0:T(8,128)(2,1)}) custom-call(bf16[576,384]{1,0:T(8,128)(2,1)} %bitcast.3, bf16[576,384]{1,0:T(8,128)(2,1)} %bitcast.5, f32[16,384,1536]{2,1,0:T(8,128)} %refs_2_.3, f32[16,1536,384]{2,1,0:T(8,128)} %refs_3_.3), custom_call_target="tpu_custom_call" | custom-call | tf_op jit(solution)/shard_map/first_pass/pallas_call | solution.py:555
  183.8 527.2 %second_pass.1 = (f32[16,384,1536]{2,1,0:T(8,128)}, f32[16,1536,384]{2,1,0:T(8,128)}, bf16[16,384,1536]{2,1,0:T(8,128)(2,1)}, bf16[16,1536,384]{2,1,0:T(8,128)(2...) custom-call(bf16[576,384]{1,0:T(8,128)(2,1)} %bitcast.4, bf16[576,384]{1,0:T(8,128)(2,1)} %bitcast.6, ...), custom_call_target="tpu_custom_call" | custom-call | tf_op jit(solution)/shard_map/second_pass/pallas_call | solution.py:554
  711.1 1.2 slice.3
  712.3 0.0 copy-start
  712.3 29.3 %copy.9 = f32[16,384,1536]{2,1,0:T(8,128)} copy(f32[16,384,1536]{2,1,0:T(8,128)} %get-tuple-element.16) | data formatting | bytes 75497472
  741.5 6.6 copy-done
  748.1 13.1 %copy.10 = f32[16,1536,384]{2,1,0:T(8,128)} copy(f32[16,1536,384]{2,1,0:T(8,128)S(1)} %copy-done) | data formatting | bytes 75497472
Async XLA Ops:
  712.3 35.8 %copy-start = (f32[16,1536,384]{2,1,0:T(8,128)S(1)}, f32[16,1536,384]{2,1,0:T(8,128)}, u32[]{:S(2)}) copy-start(f32[16,1536,384]{2,1,0:T(8,128)} %get-tuple-element.17) | copy-start | bytes 113246208

commit v3 on v2

--- a/solution.py
+++ b/solution.py
@@ -13,6 +13,7 @@
 LEARN_RATE = 8.0
 SQRT_HALF = 0.7071067811865476
 INV_SQRT_2PI = 0.3989422804014327
+HALF_LOG2E = -0.7213475204444817
 
 CHIPS = 8
 LAYERS = 16
@@ -24,6 +25,7 @@
 KB_ROWS = 768
 KB_FT = 256
 KEPT = 8
+PIECE = 144
 VMEM_LIMIT = 67043328
 
 f32, bf16 = jnp.float32, jnp.bfloat16
@@ -43,7 +45,7 @@
 
 
 def slope_tail(x):
-    return x * INV_SQRT_2PI * jnp.exp(-0.5 * x * x)
+    return x * INV_SQRT_2PI * jnp.exp2((x * x) * HALF_LOG2E)
 
 
 class Place:
@@ -161,12 +163,12 @@
 def pass_kernel(perturbed, inv_count, radius, *refs):
     if perturbed:
         (x_ref, y_ref, wi_hbm, wo_hbm, pi_own, po_own, wi_out, wo_out, wbi, wbo, u_hbm, loss_out,
-         bi, bo, hs, ds, acc, us, hg, dg, gi, go, ri, ro,
+         bi, bo, hs, ds, hm, us, hg, dg, gi, go, ri, ro,
          hsend, hrecv, dsend, drecv, usem, bsem, wsem, xsend, xrecv, sbuf, ssend, srecv,
          wi, wo, as_, ar, aps, apr, gs, gr, gps, gpr) = refs
     else:
         (x_ref, y_ref, wi_hbm, wo_hbm, wi_out, wo_out, u_hbm,
-         bi, bo, hs, ds, acc, us, hg, dg, gi, go, ri, ro,
+         bi, bo, hs, ds, hm, us, hg, dg, gi, go, ri, ro,
          hsend, hrecv, dsend, drecv, usem, bsem, wsem, xsend, xrecv, sbuf, ssend, srecv,
          si, so, fsem) = refs
     at = Place()
@@ -217,7 +219,15 @@
         return remote(src.at[span(chip), :], dst.at[span(t), :], send_sem.at[t], recv_sem.at[t], at.device(chip, at.core))
 
     def exchange(src, dst, send_sem, recv_sem):
-        each(1, CHIPS, lambda t: moved(t, src, dst, send_sem, recv_sem).start())
+        for group in ((1, 2, 4), (3, 5, 6), (7,)):
+            def step(q):
+                for t in group:
+                    chip = at.across(t)
+                    remote(src.at[pl.ds(pl.multiple_of(chip * T + q * PIECE, 16), PIECE), :],
+                           dst.at[pl.ds(pl.multiple_of(t * T + q * PIECE, 16), PIECE), :],
+                           send_sem.at[t], recv_sem.at[t], at.device(chip, at.core)).start()
+
+            each(0, T // PIECE, step)
         dst[pl.ds(0, T), :] = src[span(me), :]
 
     def weights(slot, cols):
@@ -234,8 +244,6 @@
     def get(layer):
         return pltpu.make_async_copy(u_hbm.at[layer], kept(layer), usem.at[layer % KEPT])
 
-    acc_t = acc.at[pl.ds(0, T), :]
-
     def layer_forward(layer, carry):
         slot = layer % 2
         hidden = hs[span((layer + 1) // 2), :]
@@ -246,17 +254,14 @@
             put(layer - KEPT).wait()
 
         wait(fetch(layer, slot))
+        total = hidden.astype(f32)
         for j in range(0, F, FT):
             cols = pl.ds(j, FT)
             a_w, b_w = weights(slot, cols)
             pre = dot(hidden, a_w).astype(bf16)
             pre_out[:, cols] = pre
             pre = pre.astype(f32)
-            part = dot((pre * cdf(pre)).astype(bf16), b_w)
-            if j == 0:
-                acc_t[...] = part
-            else:
-                acc_t[...] += part
+            total = total + dot((pre * cdf(pre)).astype(bf16), b_w)
 
         @pl.when(jnp.logical_and(layer >= 2, layer < KEPT))
         def _():
@@ -266,7 +271,7 @@
         def _():
             start(fetch(layer + 2, slot))
 
-        hs[span((layer + 2) // 2), :] = (hidden.astype(f32) + acc_t[...]).astype(bf16)
+        hs[span((layer + 2) // 2), :] = total.astype(bf16)
         return carry
 
     hs[pl.ds(0, T), :] = x_ref[...]
@@ -315,16 +320,13 @@
         def _():
             wait(fetch(layer, slot))
 
+        total = cot.astype(f32)
         for j in range(0, F, FT):
             cols = pl.ds(j, FT)
             a_w, b_w = weights(slot, cols)
             pre = pre_in[:, cols].astype(f32)
             err = (dot(cot, b_w, NT) * (cdf(pre) + slope_tail(pre))).astype(bf16)
-            part = dot(err, a_w, NT)
-            if j == 0:
-                acc_t[...] = part
-            else:
-                acc_t[...] += part
+            total = total + dot(err, a_w, NT)
 
         @pl.when(layer >= KEPT + 2)
         def _():
@@ -338,7 +340,7 @@
         def _():
             start(fetch(me * 2 + 3 - layer, slot))
 
-        ds[span((layer - 2) // 2), :] = (cot.astype(f32) + acc_t[...]).astype(bf16)
+        ds[span((layer - 2) // 2), :] = total.astype(bf16)
         return carry
 
     lax.fori_loop(0, LAYERS - 2, layer_backward, 0)
@@ -372,22 +374,22 @@
         arrive(i, hs, hg, hsend, hrecv)
         rows = block(i)
         h_low = hg[rows, :]
-        acc[...] = h_low.astype(f32)
-        for j in range(0, F, KB_FT):
-            cols = pl.ds(j, KB_FT)
+        total = h_low.astype(f32)
+        for j in range(0, F, FT):
+            cols = pl.ds(j, FT)
             pre = dot(h_low, bi[low, :, cols]).astype(bf16)
             us[rows, cols] = pre
             pre = pre.astype(f32)
-            acc[...] += dot((pre * cdf(pre)).astype(bf16), bo[low, cols, :])
-        hs[rows, :] = acc[...].astype(bf16)
+            total = total + dot((pre * cdf(pre)).astype(bf16), bo[low, cols, :])
+        hm[rows, :] = total.astype(bf16)
         return carry
 
     def sweep_high(i, carry):
         arrive(i, ds, dg, dsend, drecv)
         rows = block(i)
-        h_mid, d_top = hs[rows, :], dg[rows, :]
+        h_mid, d_top = hm[rows, :], dg[rows, :]
         h_mid_t, d_top_t = h_mid.T, d_top.T
-        acc[...] = d_top.astype(f32)
+        total = d_top.astype(f32)
         for j in range(0, F, KB_FT):
             cols = pl.ds(j, KB_FT)
             pre = dot(h_mid, bi[high, :, cols]).astype(bf16).astype(f32)
@@ -396,8 +398,8 @@
             err = (dot(d_top, bo[high, cols, :], NT) * (half + slope_tail(pre))).astype(bf16)
             add(i, go, 1, cols, dot(d_top_t, post))
             add(i, gi, 1, cols, dot(h_mid_t, err))
-            acc[...] += dot(err, bi[high, :, cols], NT)
-        dg[rows, :] = acc[...].astype(bf16)
+            total = total + dot(err, bi[high, :, cols], NT)
+        dg[rows, :] = total.astype(bf16)
         return carry
 
     def sweep_back(i, carry):
@@ -469,7 +471,6 @@
 
     blocks = ROWS // KB_ROWS
     take(me * 2, low)
-    each(1, CHIPS, lambda t: moved(t, hs, hg, hsend, hrecv).wait_send())
     lax.fori_loop(0, blocks, sweep_low, 0)
     take(me * 2 + 1, high)
     if not perturbed:
@@ -486,7 +487,11 @@
     def _():
         start(swap(0))
 
-    each(1, CHIPS, lambda t: moved(t, ds, dg, dsend, drecv).wait_send())
+    def sent(t):
+        moved(t, hs, hg, hsend, hrecv).wait_send()
+        moved(t, ds, dg, dsend, drecv).wait_send()
+
+    each(1, CHIPS, sent)
     if perturbed:
         @pl.when(at.core == 0)
         def _():
@@ -526,7 +531,7 @@
     acts = ((LAYERS, T, F), bf16)
     scratch = [
         pltpu.VMEM((2, D, F), bf16), pltpu.VMEM((2, F, D), bf16),
-        pltpu.VMEM((ROWS + T, D), bf16), pltpu.VMEM((ROWS, D), bf16), pltpu.VMEM((KB_ROWS, D), f32), pltpu.VMEM((ROWS, F), bf16),
+        pltpu.VMEM((ROWS + T, D), bf16), pltpu.VMEM((ROWS, D), bf16), pltpu.VMEM((ROWS, D), bf16), pltpu.VMEM((ROWS, F), bf16),
         pltpu.VMEM((ROWS, D), bf16), pltpu.VMEM((ROWS, D), bf16),
         pltpu.VMEM((2, D, F), f32), pltpu.VMEM((2, D, F), f32), pltpu.VMEM((D, F), f32), pltpu.VMEM((D, F), f32),
         DMA((CHIPS,)), DMA((CHIPS,)), DMA((CHIPS,)), DMA((CHIPS,)), DMA((KEPT,)), DMA((2, 2)), DMA((4,)), DMA((2,)), DMA((2,)),

time: 769 us -> 747 us (0.971)
  Pallas kernels: 710 us -> 690 us
    pallas_call x1, Pallas kernels: 183 us -> 172 us  [one_pass(): return pl.pallas_call(kernel, **options)(x, y, w_in, w_out)]
    pallas_call x1, Pallas kernels: 527 us -> 518 us  [one_pass(): return pl.pallas_call(kernel, **options)(x, y, w_in, w_out, *pert)]
where the time goes in v3:
time: 747 us; the launch traced here: 741 us
  Pallas kernels  690 us (92%)
  local copies, waits for them, and re-layouts  50.1 us (7%)
    pallas_call x1, Pallas kernels, one_pass(): return pl.pallas_call(kernel, **options)(x, y, w_in, w_out, *pert)  518 us
    pallas_call x1, Pallas kernels, one_pass(): return pl.pallas_call(kernel, **options)(x, y, w_in, w_out)  172 us
    unnamed x4, local copies, waits for them, and re-layouts  48.9 us

profile of v3, /device:TPU:1, one launch (start us, length us, event | category | flops | bytes accessed | tf_op | source)
XLA Modules:
  0.0 741.4 jit_solution(10706614908193822099)
XLA Ops:
  0.6 172.0 %first_pass.1 = (bf16[384,1536]{1,0:T(8,128)(2,1)}, bf16[1536,384]{1,0:T(8,128)(2,1)}, bf16[16,576,1536]{2,1,0:T(8,128)(2,1)}) custom-call(bf16[576,384]{1,0:T(8,128)(2,1)} %bitcast.3, bf16[576,384]{1,0:T(8,128)(2,1)} %bitcast.5, f32[16,384,1536]{2,1,0:T(8,128)} %refs_2_.3, f32[16,1536,384]{2,1,0:T(8,128)} %refs_3_.3), custom_call_target="tpu_custom_call" | custom-call | tf_op jit(solution)/shard_map/first_pass/pallas_call | solution.py:560
  172.6 518.1 %second_pass.1 = (f32[16,384,1536]{2,1,0:T(8,128)}, f32[16,1536,384]{2,1,0:T(8,128)}, bf16[16,384,1536]{2,1,0:T(8,128)(2,1)}, bf16[16,1536,384]{2,1,0:T(8,128)(2...) custom-call(bf16[576,384]{1,0:T(8,128)(2,1)} %bitcast.4, bf16[576,384]{1,0:T(8,128)(2,1)} %bitcast.6, ...), custom_call_target="tpu_custom_call" | custom-call | tf_op jit(solution)/shard_map/second_pass/pallas_call | solution.py:559
  690.8 1.2 slice.3
  692.0 0.0 copy-start
  692.0 29.3 %copy.9 = f32[16,384,1536]{2,1,0:T(8,128)} copy(f32[16,384,1536]{2,1,0:T(8,128)} %get-tuple-element.16) | data formatting | bytes 75497472
  721.2 6.6 copy-done
  727.8 13.1 %copy.10 = f32[16,1536,384]{2,1,0:T(8,128)} copy(f32[16,1536,384]{2,1,0:T(8,128)S(1)} %copy-done) | data formatting | bytes 75497472
Async XLA Ops:
  692.0 35.8 %copy-start = (f32[16,1536,384]{2,1,0:T(8,128)S(1)}, f32[16,1536,384]{2,1,0:T(8,128)}, u32[]{:S(2)}) copy-start(f32[16,1536,384]{2,1,0:T(8,128)} %get-tuple-element.17) | copy-start | bytes 113246208

commit v4 on v3

--- a/solution.py
+++ b/solution.py
@@ -48,29 +48,41 @@
     return x * INV_SQRT_2PI * jnp.exp2((x * x) * HALF_LOG2E)
 
 
+def div(a, b):
+    return lax.div(jnp.int32(a), jnp.int32(b))
+
+
+def rem(a, b):
+    return lax.rem(jnp.int32(a), jnp.int32(b))
+
+
+def some(k):
+    return div(k * k + 35, 36)
+
+
+def bit(dim):
+    return 1 + dim + div(dim * (dim - 1), 2)
+
+
 class Place:
     def __init__(self):
         self.z, self.y, data = lax.axis_index("model"), lax.axis_index("sub"), lax.axis_index("data")
-        self.x, self.core = data // 2, data % 2
+        self.x, self.core = div(data, 2), rem(data, 2)
         self.chip = self.z * 4 + self.y * 2 + self.x
         self.mine = self.chip * 2 + self.core
 
     def across(self, t):
-        x, y, z = (self.x + t) % 2, (self.y + t // 2) % 2, (self.z + t // 4) % 2
+        x, y, z = rem(self.x + t, 2), rem(self.y + div(t, 2), 2), rem(self.z + div(t, 4), 2)
         return z * 4 + y * 2 + x
 
     def device(self, chip, core):
-        return (chip // 4, (chip // 2) % 2, (chip % 2) * 2 + core)
+        return (div(chip, 4), rem(div(chip, 2), 2), rem(chip, 2) * 2 + core)
 
     def partner(self):
         return self.device(self.chip, 1 - self.core)
 
     def peer(self, i):
-        return self.device(self.across(i // 2), (self.core + i) % 2)
-
-
-def bit(dim):
-    return 1 + dim + dim * (dim - 1) // 2
+        return self.device(self.across(div(i, 2)), rem(self.core + i, 2))
 
 
 def each(first, last, body):
@@ -94,8 +106,6 @@
 
 
 class Gather:
-    MESSAGES = ((0, ()), (1, ()), (2, ()), (1, (1,)), (2, (2,)), (2, (1,)), (2, (1, 2)))
-
     def __init__(self, at, tensors, send, recv, pair_send, pair_recv):
         self.at, self.tensors = at, tensors
         self.sems = (send, recv, pair_send, pair_recv)
@@ -108,56 +118,65 @@
         return remote(ref.at[rows, :] if own else dst, dst, send, recv, device)
 
     def parts(self, dim, slot):
-        back, turns = self.MESSAGES[slot]
-        t = 0
-        for o in turns:
-            t = t + bit((dim + 3 - o) % 3)
-        return (dim + 3 - back) % 3, t
-
-    def link(self, i, dim, slot):
-        part, t = self.parts(dim, slot)
+        later = some(slot) * some(slot - 1) * some(slot - 2)
+        back = some(slot) + some(slot) * some(slot - 1) - 1 + some(slot - 3)
+        one, two = later * some(slot - 4), later * (1 - rem(slot, 2))
+        return rem(dim + 3 - back, 3), one * bit(rem(dim + 2, 3)) + two * bit(rem(dim + 1, 3))
+
+    def link(self, i, dim, slot, own=False):
+        part, t = (rem(dim + 3 - slot, 3), 0) if own else self.parts(dim, slot)
         send, recv, _, _ = self.sems
-        return self.make(i, part, slot < 3, self.at.across(t) if slot >= 3 else self.at.chip, send.at[dim, slot, i],
-                         recv.at[dim, slot, i], self.at.device(self.at.across(bit(dim)), self.at.core))
+        index = slot * 3 + dim
+        return self.make(i, part, own, self.at.chip if own else self.at.across(t), send.at[index, i], recv.at[index, i],
+                         self.at.device(self.at.across(bit(dim)), self.at.core))
 
     def pair(self, i, part, own, chip, index):
         _, _, send, recv = self.sems
         return self.make(i, part, own, chip, send.at[index, i], recv.at[index, i], self.at.partner())
 
+    def passing(self, i, index, which):
+        return self.make(i, 0, False, self.at.chip, self.sems[which].at[index, i], self.sems[which + 1].at[index, i], self.at.partner())
+
     def start(self):
-        for slot in range(3):
+        def own(slot):
             for i in range(2):
-                each(0, 3, lambda dim: self.link(i, dim, slot).start())
+                each(0, 3, lambda dim: self.link(i, dim, slot, own=True).start())
+
+        each(0, 3, own)
         for i in range(2):
             each(0, 3, lambda part: self.pair(i, part, True, self.at.chip, part).start())
 
     def run(self):
-        turn = {0: (3, 1), 1: (5, 1), 3: (6, 1)}
-        for slot in range(7):
+        def step(slot):
             for i in range(2):
                 def got(dim):
-                    self.link(i, dim, slot).wait_recv()
-                    if slot in turn:
-                        later, step = turn[slot]
-                        self.link(i, (dim + step) % 3, later).start()
+                    self.passing(i, slot * 3 + dim, 0).wait_recv()
+
+                    @pl.when(jnp.logical_or(slot <= 1, slot == 3))
+                    def _():
+                        self.link(i, rem(dim + 1, 3), 3 + 2 * some(slot) + div(slot, 3)).start()
+
                     part, t = self.parts(dim, slot)
                     self.pair(i, part, False, self.at.across(t + bit(dim)), 3 + slot * 3 + dim).start()
 
                 each(0, 3, got)
-            if slot == 0:
+
+            @pl.when(slot == 0)
+            def _():
                 for i in range(2):
                     each(0, 3, lambda dim: self.link(i, dim, 4).start())
+
+        each(0, 7, step)
         for i in range(2):
-            each(0, 24, lambda index: self.pair(i, 0, False, self.at.chip, index).wait_recv())
+            each(0, 24, lambda index: self.passing(i, index, 2).wait_recv())
 
     def finish(self):
         for i in range(2):
-            each(0, 24, lambda index: self.pair(i, 0, False, self.at.chip, index).wait_send())
-            for slot in range(7):
-                each(0, 3, lambda dim: self.link(i, dim, slot).wait_send())
-
-
-GATHER_SEMS = [DMA((3, 7, 2)), DMA((3, 7, 2)), DMA((24, 2)), DMA((24, 2))]
+            each(0, 24, lambda index: self.passing(i, index, 2).wait_send())
+            each(0, 21, lambda index: self.passing(i, index, 0).wait_send())
+
+
+GATHER_SEMS = [DMA((21, 2)), DMA((21, 2)), DMA((24, 2)), DMA((24, 2))]
 
 
 def pass_kernel(perturbed, inv_count, radius, *refs):
@@ -411,14 +430,24 @@
         rows = block(i)
         h_low, d_mid = hg[rows, :], dg[rows, :]
         h_low_t, d_mid_t = h_low.T, d_mid.T
-        for j in range(0, F, KB_FT):
-            cols = pl.ds(j, KB_FT)
+
+        def columns(cols):
             pre = us[rows, cols].astype(f32)
             half = cdf(pre)
             post = (pre * half).astype(bf16)
             err = (dot(d_mid, bo[low, cols, :], NT) * (half + slope_tail(pre))).astype(bf16)
             add(i, go, 0, cols, dot(d_mid_t, post))
             add(i, gi, 0, cols, dot(h_low_t, err))
+
+        if perturbed:
+            def part(p):
+                for j in range(0, F // 2, KB_FT):
+                    columns(pl.ds(pl.multiple_of(p * (F // 2) + j, KB_FT), KB_FT))
+
+            each(0, 2, part)
+        else:
+            for j in range(0, F, KB_FT):
+                columns(pl.ds(j, KB_FT))
         return carry
 
     def swap(which):

time: 747 us -> 740 us (level)
  no operation moved by 1% of the time
where the time goes in v4:
time: 740 us; the launch traced here: 739 us
  Pallas kernels  689 us (93%)
  local copies, waits for them, and re-layouts  50.1 us (7%)
    pallas_call x1, Pallas kernels, one_pass(): return pl.pallas_call(kernel, **options)(x, y, w_in, w_out, *pert)  517 us
    pallas_call x1, Pallas kernels, one_pass(): return pl.pallas_call(kernel, **options)(x, y, w_in, w_out)  172 us
    unnamed x4, local copies, waits for them, and re-layouts  48.9 us

profile of v4, /device:TPU:1, one launch (start us, length us, event | category | flops | bytes accessed | tf_op | source)
XLA Modules:
  0.0 739.4 jit_solution(5382414140222083015)
XLA Ops:
  0.6 171.6 %first_pass.1 = (bf16[384,1536]{1,0:T(8,128)(2,1)}, bf16[1536,384]{1,0:T(8,128)(2,1)}, bf16[16,576,1536]{2,1,0:T(8,128)(2,1)}) custom-call(bf16[576,384]{1,0:T(8,128)(2,1)} %bitcast.3, bf16[576,384]{1,0:T(8,128)(2,1)} %bitcast.5, f32[16,384,1536]{2,1,0:T(8,128)} %refs_2_.3, f32[16,1536,384]{2,1,0:T(8,128)} %refs_3_.3), custom_call_target="tpu_custom_call" | custom-call | tf_op jit(solution)/shard_map/first_pass/pallas_call | solution.py:589
  172.2 517.1 %second_pass.1 = (f32[16,384,1536]{2,1,0:T(8,128)}, f32[16,1536,384]{2,1,0:T(8,128)}, bf16[16,384,1536]{2,1,0:T(8,128)(2,1)}, bf16[16,1536,384]{2,1,0:T(8,128)(2...) custom-call(bf16[576,384]{1,0:T(8,128)(2,1)} %bitcast.4, bf16[576,384]{1,0:T(8,128)(2,1)} %bitcast.6, ...), custom_call_target="tpu_custom_call" | custom-call | tf_op jit(solution)/shard_map/second_pass/pallas_call | solution.py:588
  689.3 1.2 slice.3
  690.5 0.0 copy-start
  690.5 29.3 %copy.9 = f32[16,384,1536]{2,1,0:T(8,128)} copy(f32[16,384,1536]{2,1,0:T(8,128)} %get-tuple-element.16) | data formatting | bytes 75497472
  719.8 6.6 copy-done
  726.3 13.1 %copy.10 = f32[16,1536,384]{2,1,0:T(8,128)} copy(f32[16,1536,384]{2,1,0:T(8,128)S(1)} %copy-done) | data formatting | bytes 75497472
Async XLA Ops:
  690.5 35.8 %copy-start = (f32[16,1536,384]{2,1,0:T(8,128)S(1)}, f32[16,1536,384]{2,1,0:T(8,128)}, u32[]{:S(2)}) copy-start(f32[16,1536,384]{2,1,0:T(8,128)} %get-tuple-element.17) | copy-start | bytes 113246208

commit v5 on v4

--- a/solution.py
+++ b/solution.py
@@ -93,10 +93,13 @@
     lax.fori_loop(first, last, step, 0)
 
 
-def meet(at):
+def greet(at):
     barrier = pltpu.get_barrier_semaphore()
     each(1, 16, lambda i: pl.semaphore_signal(barrier, inc=1, device_id=at.peer(i), device_id_type=MESH))
-    pl.semaphore_wait(barrier, 15)
+
+
+def met():
+    pl.semaphore_wait(pltpu.get_barrier_semaphore(), 15)
 
 
 def remote(src, dst, send_sem, recv_sem, device):
@@ -181,15 +184,15 @@
 
 def pass_kernel(perturbed, inv_count, radius, *refs):
     if perturbed:
-        (x_ref, y_ref, wi_hbm, wo_hbm, pi_own, po_own, wi_out, wo_out, wbi, wbo, u_hbm, loss_out,
+        (x_ref, y_ref, wi_hbm, wo_hbm, wbi, wbo, wi_out, wo_out, u_hbm, loss_out,
          bi, bo, hs, ds, hm, us, hg, dg, gi, go, ri, ro,
          hsend, hrecv, dsend, drecv, usem, bsem, wsem, xsend, xrecv, sbuf, ssend, srecv,
-         wi, wo, as_, ar, aps, apr, gs, gr, gps, gpr) = refs
+         gs, gr, gps, gpr, wi, wo) = refs
     else:
-        (x_ref, y_ref, wi_hbm, wo_hbm, wi_out, wo_out, u_hbm,
+        (x_ref, y_ref, wi_hbm, wo_hbm, wbi, wbo, u_hbm,
          bi, bo, hs, ds, hm, us, hg, dg, gi, go, ri, ro,
          hsend, hrecv, dsend, drecv, usem, bsem, wsem, xsend, xrecv, sbuf, ssend, srecv,
-         si, so, fsem) = refs
+         gs, gr, gps, gpr, si, so, fsem) = refs
     at = Place()
     me = at.chip
     mine = at.mine
@@ -214,21 +217,11 @@
 
     own_w = [pltpu.make_async_copy(wi_hbm.at[mine], wi if perturbed else si.at[0], wsem.at[0]),
              pltpu.make_async_copy(wo_hbm.at[mine], wo if perturbed else so.at[0], wsem.at[1])]
-    if perturbed:
-        keep = [pltpu.make_async_copy(pi_own, wbi.at[mine], wsem.at[2]), pltpu.make_async_copy(po_own, wbo.at[mine], wsem.at[3])]
-        start(keep)
+    for layer in range(2):
+        start(fetch(layer, layer))
+    if perturbed:
         start(own_w)
-        meet(at)
-        spread = Gather(at, [(pi_own, wbi), (po_own, wbo)], as_, ar, aps, apr)
-        spread.start()
-        spread.run()
-        wait(keep)
-        for layer in range(2):
-            start(fetch(layer, layer))
-    else:
-        for layer in range(2):
-            start(fetch(layer, layer))
-        meet(at)
+    greet(at)
 
     def span(k):
         return pl.ds(pl.multiple_of(k * T, T), T)
@@ -295,6 +288,7 @@
 
     hs[pl.ds(0, T), :] = x_ref[...]
     lax.fori_loop(0, LAYERS, layer_forward, 0)
+    met()
     exchange(hs, hg, hsend, hrecv)
 
     def share(value):
@@ -489,8 +483,11 @@
         return lax.fori_loop(0, F // C, sum_out, total)
 
     if perturbed:
-        gather = Gather(at, [(wi, wi_out), (wo, wo_out)], gs, gr, gps, gpr)
-        keep_new = [pltpu.make_async_copy(wi, wi_out.at[mine], wsem.at[0]), pltpu.make_async_copy(wo, wo_out.at[mine], wsem.at[1])]
+        new = [(wi, wi_out), (wo, wo_out)]
+    else:
+        new = [(bi.at[0], wbi), (bo.at[0], wbo)]
+    gather = Gather(at, new, gs, gr, gps, gpr)
+    keep_new = [pltpu.make_async_copy(own, slots.at[mine], wsem.at[2 + i]) for i, (own, slots) in enumerate(new)]
 
     def update():
         wait(own_w)
@@ -526,11 +523,7 @@
         def _():
             update()
 
-        gather.run()
-        loss_out[...] = share_finish() * inv_count
-        spread.finish()
-        gather.finish()
-        wait(keep_new)
+        loss_out[0] = jnp.max(share_finish() * inv_count)
     else:
         wait(own_w)
         sbuf[mine] = sum_layer()
@@ -549,9 +542,12 @@
 
         lax.fori_loop(0, D // R, perturb_in, 0)
         lax.fori_loop(0, F // C, perturb_out, 0)
-        done = [pltpu.make_async_copy(bi.at[0], wi_out, wsem.at[2]), pltpu.make_async_copy(bo.at[0], wo_out, wsem.at[3])]
-        start(done)
-        wait(done)
+        gather.start()
+        start(keep_new)
+
+    gather.run()
+    gather.finish()
+    wait(keep_new)
     for c in swap(0):
         c.wait_send()
 
@@ -567,16 +563,16 @@
         pltpu.VMEM((LAYERS, 8, 128), f32), DMA((LAYERS,)), DMA((LAYERS,)),
     ]
     if perturbed:
-        shapes = [((LAYERS, D, F), f32), ((LAYERS, F, D), f32), ((LAYERS, D, F), bf16), ((LAYERS, F, D), bf16), acts, ((8, 128), f32)]
-        out_specs = [ANY] * 5 + [V]
-        scratch += [pltpu.VMEM((D, F), f32), pltpu.VMEM((F, D), f32), *GATHER_SEMS, *GATHER_SEMS]
+        shapes = [((LAYERS, D, F), f32), ((LAYERS, F, D), f32), acts, ((1,), f32)]
+        out_specs = [ANY] * 3 + [pl.BlockSpec(memory_space=pltpu.SMEM)]
+        scratch += [*GATHER_SEMS, pltpu.VMEM((D, F), f32), pltpu.VMEM((F, D), f32)]
     else:
-        shapes = [((D, F), bf16), ((F, D), bf16), acts]
+        shapes = [((LAYERS, D, F), bf16), ((LAYERS, F, D), bf16), acts]
         out_specs = [ANY] * 3
-        scratch += [pltpu.VMEM((2, D, F), f32), pltpu.VMEM((2, F, D), f32), DMA((2, 2))]
+        scratch += [*GATHER_SEMS, pltpu.VMEM((2, D, F), f32), pltpu.VMEM((2, F, D), f32), DMA((2, 2))]
     options = dict(
         out_shape=[jax.ShapeDtypeStruct(*s) for s in shapes],
-        in_specs=[V, V, ANY, ANY] + [V] * len(pert),
+        in_specs=[V, V, ANY, ANY] + [ANY] * len(pert),
         out_specs=out_specs,
         scratch_shapes=scratch,
         compiler_params=pltpu.CompilerParams(
@@ -600,7 +596,7 @@
         radius = RHO_REL * math.sqrt(layers * hidden_dim + model_dim)
         x, y = images.reshape(T, D), targets.reshape(T, D)
         pert = one_pass(False, inv_count, radius, x, y, w_in, w_out)[:2]
-        new_in, new_out, _, _, _, loss = one_pass(True, inv_count, radius, x, y, w_in, w_out, pert)
-        return new_in, new_out, loss[0, 0]
+        new_in, new_out, _, loss = one_pass(True, inv_count, radius, x, y, w_in, w_out, pert)
+        return new_in, new_out, loss.reshape(())
 
     return jax.shard_map(local_step, mesh=mesh, in_specs=(batch_spec, batch_spec, P(), P()), out_specs=(P(), P(), P()), check_vma=False)

time: 740 us -> 738 us (level)
    pallas_call x1, Pallas kernels: 517 us -> 390 us  [one_pass(): return pl.pallas_call(kernel, **options)(x, y, w_in, w_out, *pert)]
    pallas_call x1, Pallas kernels: 172 us -> 296 us  [one_pass(): return pl.pallas_call(kernel, **options)(x, y, w_in, w_out)]
where the time goes in v5:
time: 738 us; the launch traced here: 737 us
  Pallas kernels  686 us (93%)
  local copies, waits for them, and re-layouts  48.9 us (7%)
    pallas_call x1, Pallas kernels, one_pass(): return pl.pallas_call(kernel, **options)(x, y, w_in, w_out, *pert)  390 us
    pallas_call x1, Pallas kernels, one_pass(): return pl.pallas_call(kernel, **options)(x, y, w_in, w_out)  296 us
    unnamed x4, local copies, waits for them, and re-layouts  48.9 us

profile of v5, /device:TPU:1, one launch (start us, length us, event | category | flops | bytes accessed | tf_op | source)
XLA Modules:
  0.0 737.4 jit_solution(16221991658219902741)
XLA Ops:
  0.6 295.8 %first_pass.1 = (bf16[16,384,1536]{2,1,0:T(8,128)(2,1)}, bf16[16,1536,384]{2,1,0:T(8,128)(2,1)}, bf16[16,576,1536]{2,1,0:T(8,128)(2,1)}) custom-call(bf16[576,384]{1,0:T(8,128)(2,1)} %bitcast.3, bf16[576,384]{1,0:T(8,128)(2,1)} %bitcast.5, f32[16,384,1536]{2,1,0:T(8,128)} %refs_2_.3, f32[16,1536,384]{2,1,0:T(8,128)} %refs_3_.3), custom_call_target="tpu_custom_call" | custom-call | tf_op jit(solution)/shard_map/first_pass/pallas_call | solution.py:585
  296.4 390.3 %second_pass.1 = (f32[16,384,1536]{2,1,0:T(8,128)}, f32[16,1536,384]{2,1,0:T(8,128)}, bf16[16,576,1536]{2,1,0:T(8,128)(2,1)}, f32[1]{0:T(128)}) custom-call(bf16[576,384]{1,0:T(8,128)(2,1)} %bitcast.4, bf16[576,384]{1,0:T(8,128)(2,1)} %bitcast.6, f32[16,384,1536]{2,1,0:T(8,128)} %refs_2_.3, f32[16,1536,384]{2,1,0:T(8,128)} %refs_3_.3, ...), custom_call_target="tpu_custom_call" | custom-call | tf_op jit(solution)/shard_map/second_pass/pallas_call | solution.py:584
  686.7 0.0 copy-start
  686.8 29.3 %copy.10 = f32[16,384,1536]{2,1,0:T(8,128)} copy(f32[16,384,1536]{2,1,0:T(8,128)} %get-tuple-element.16) | data formatting | bytes 75497472
  716.0 6.5 copy-done
  722.6 13.1 %copy.11 = f32[16,1536,384]{2,1,0:T(8,128)} copy(f32[16,1536,384]{2,1,0:T(8,128)S(1)} %copy-done) | data formatting | bytes 75497472
Async XLA Ops:
  686.7 35.8 %copy-start = (f32[16,1536,384]{2,1,0:T(8,128)S(1)}, f32[16,1536,384]{2,1,0:T(8,128)}, u32[]{:S(2)}) copy-start(f32[16,1536,384]{2,1,0:T(8,128)} %get-tuple-element.17) | copy-start | bytes 113246208

commit v6 on v5

--- a/solution.py
+++ b/solution.py
@@ -528,6 +528,13 @@
         wait(own_w)
         sbuf[mine] = sum_layer()
         share_start()
+
+        def turn(i, carry):
+            cols = pl.ds(pl.multiple_of(i * C, C), C)
+            so[1, cols, :] = ro[:, cols].T
+            return carry
+
+        lax.fori_loop(0, F // C, turn, 0)
         scale = radius / jnp.sqrt(jnp.sum(share_finish(), axis=(0, 1), keepdims=True))
 
         def perturb_in(i, carry):
@@ -537,7 +544,7 @@
 
         def perturb_out(i, carry):
             cols = pl.ds(pl.multiple_of(i * C, C), C)
-            bo[0, cols, :] = (so[0, cols, :] + scale * ro[:, cols].T).astype(bf16)
+            bo[0, cols, :] = (so[0, cols, :] + scale * so[1, cols, :]).astype(bf16)
             return carry
 
         lax.fori_loop(0, D // R, perturb_in, 0)

time: 738 us -> 736 us (level)
  no operation moved by 1% of the time
where the time goes in v6:
time: 736 us
  Pallas kernels  685 us (93%)
  local copies, waits for them, and re-layouts  48.9 us (7%)
    pallas_call x1, Pallas kernels, one_pass(): return pl.pallas_call(kernel, **options)(x, y, w_in, w_out, *pert)  390 us
    pallas_call x1, Pallas kernels, one_pass(): return pl.pallas_call(kernel, **options)(x, y, w_in, w_out)  294 us
    unnamed x4, local copies, waits for them, and re-layouts  48.9 us

profile of v6, /device:TPU:1, one launch (start us, length us, event | category | flops | bytes accessed | tf_op | source)
XLA Modules:
  0.0 736.2 jit_solution(11111708961649229743)
XLA Ops:
  0.6 294.4 %first_pass.1 = (bf16[16,384,1536]{2,1,0:T(8,128)(2,1)}, bf16[16,1536,384]{2,1,0:T(8,128)(2,1)}, bf16[16,576,1536]{2,1,0:T(8,128)(2,1)}) custom-call(bf16[576,384]{1,0:T(8,128)(2,1)} %bitcast.3, bf16[576,384]{1,0:T(8,128)(2,1)} %bitcast.5, f32[16,384,1536]{2,1,0:T(8,128)} %refs_2_.3, f32[16,1536,384]{2,1,0:T(8,128)} %refs_3_.3), custom_call_target="tpu_custom_call" | custom-call | tf_op jit(solution)/shard_map/first_pass/pallas_call | solution.py:592
  295.0 390.5 %second_pass.1 = (f32[16,384,1536]{2,1,0:T(8,128)}, f32[16,1536,384]{2,1,0:T(8,128)}, bf16[16,576,1536]{2,1,0:T(8,128)(2,1)}, f32[1]{0:T(128)}) custom-call(bf16[576,384]{1,0:T(8,128)(2,1)} %bitcast.4, bf16[576,384]{1,0:T(8,128)(2,1)} %bitcast.6, f32[16,384,1536]{2,1,0:T(8,128)} %refs_2_.3, f32[16,1536,384]{2,1,0:T(8,128)} %refs_3_.3, ...), custom_call_target="tpu_custom_call" | custom-call | tf_op jit(solution)/shard_map/second_pass/pallas_call | solution.py:591
  685.5 0.0 copy-start
  685.5 29.3 %copy.10 = f32[16,384,1536]{2,1,0:T(8,128)} copy(f32[16,384,1536]{2,1,0:T(8,128)} %get-tuple-element.16) | data formatting | bytes 75497472
  714.8 6.5 copy-done
  721.4 13.1 %copy.11 = f32[16,1536,384]{2,1,0:T(8,128)} copy(f32[16,1536,384]{2,1,0:T(8,128)S(1)} %copy-done) | data formatting | bytes 75497472
Async XLA Ops:
  685.5 35.8 %copy-start = (f32[16,1536,384]{2,1,0:T(8,128)S(1)}, f32[16,1536,384]{2,1,0:T(8,128)}, u32[]{:S(2)}) copy-start(f32[16,1536,384]{2,1,0:T(8,128)} %get-tuple-element.17) | copy-start | bytes 113246208
